TPU v7x, 128 devices: a whole 4x4x4 slice. The times are simulated.
128 devices in a mesh: freq: 64 (over x, y, z_hi, core), depth: 2 (over z_lo).
Axes of the slice: x: 4, y: 4, z: 4 (z_hi: 2, z_lo: 2; z = z_hi * 2 + z_lo), core: 2. Of those that a mesh axis runs over, the one named last changes fastest.
Arguments:
- pressure_field: bfloat16 [8192, 16384], P('depth', 'freq'), may hold values from -6 to 6
- block_main: bfloat16 [8192, 3, 2, 128], P('depth'), may hold values from -0.15625 to 0.15625
- block_coupled: bfloat16 [8192, 3, 2, 128], P('depth'), may hold values from -0.15625 to 0.15625
- coupling: float32 [16384], P('freq'), may hold values from -3 to 3
- frequencies: float32 [8192], replicated, may hold values from 1 to 1024
- receivers: int32 [512], replicated, may hold values from 0 to 8191
- floors: int32 [4], replicated, may hold values from 2048 to 8191
Outputs:
- series: float32 [512, 2048], P('depth', 'freq')
Inputs may be any that keep to these rules, and one draw needn't show every extreme that they name: `receivers`: any depth cells, repeats possible.
All inputs are finite; a program needn't handle non-finite values.
Results may differ from a plain program's by a relative error of at most 0.0061.
Values may be sent and summed in bfloat16 or wider, within the bound.
A program may use at most 256 MiB of HBM per device.

v0:
```python
import functools
import math

import jax
import jax.numpy as jnp
from jax import lax
from jax.experimental import pallas as pl
from jax.experimental.pallas import tpu as pltpu
from jax.sharding import PartitionSpec as P

NT = 2048
STEPS = 4

COS_TERMS = (1.0, -19.739208221435547, 64.93939208984375, -85.45665740966797,
             60.242130279541016, -26.4046688079834, 7.800131320953369, -1.453112244606018)
SIN_TERMS = (6.2831854820251465, -41.34170150756836, 81.6052474975586, -76.70580291748047,
             42.05775451660156, -15.086565017700195, 3.7813189029693604, -0.6207787394523621)

MESH = pl.DeviceIdType.MESH
F32 = jnp.float32
BF16 = jnp.bfloat16


def poly(terms, z):
    total = jnp.full_like(z, terms[-1])
    for term in terms[-2::-1]:
        total = total * z + F32(term)
    return total


def unroll_of(count, choices=(5, 4, 3, 2, 1)):
    return next(c for c in choices if count % c == 0)


def split_rows(rows, parts):
    unit = 16
    units = rows // unit
    cuts = [round(units * i / parts) * unit for i in range(parts)] + [rows]
    return [(cuts[i], cuts[i + 1] - cuts[i]) for i in range(parts)]


def plan_of(rows, bits):
    parts = min(3, max(1, bits - 1))
    plan = []
    for i, (start, count) in enumerate(split_rows(rows, parts)):
        low = list(range(bits - 1))
        order = low[i:] + low[:i] + [bits - 1]
        plan.append((start, count, order))
    return plan


def kernel(depth_n, freq_n, bits, factor, plan,
           field, main_hbm, side_hbm, weights, freqs, receivers, floors, out,
           raw_main, raw_side, spread, ops, w_buf, final, halo, picked, owned, pick_in,
           basis, sums, *rest):
    n_parts = len(plan)
    send_bufs = rest[:n_parts]
    recv_bufs = rest[n_parts:2 * n_parts]
    load_sem, halo_send, halo_recv, pick_send, pick_recv, rs_send, rs_recv = rest[2 * n_parts:]
    rows, width = field.shape
    half = width // 2
    bs = raw_main.shape[1]
    kc = 6
    nb = rows // bs
    bw = 2 * bs
    me_d = lax.axis_index("depth")
    me_f = lax.axis_index("freq")
    first_row = me_d * rows

    for which, (src, dst) in enumerate(((main_hbm, raw_main), (side_hbm, raw_side))):
        def start(b, carry, src=src, dst=dst, which=which):
            at = pl.ds(pl.multiple_of(b * kc * bs, kc * bs), kc * bs)
            pltpu.make_async_copy(src.at[at], dst.at[at], load_sem.at[which, b]).start()
            return carry
        lax.fori_loop(0, nb, start, 0)

    barrier = pltpu.get_barrier_semaphore()
    for off in range(1, depth_n):
        pl.semaphore_signal(barrier, inc=1, device_id={"depth": lax.rem(me_d + off, depth_n)},
                            device_id_type=MESH)
    partners = []
    for j in range(bits):
        mine = lax.rem(me_f // (1 << j), 2)
        partners.append((mine, me_f + (1 - 2 * mine) * (1 << j)))
        pl.semaphore_signal(barrier, inc=1, device_id={"freq": partners[j][1]}, device_id_type=MESH)

    def put_w(parity, b, re, im):
        base = pl.multiple_of((b + 1) * bw, bw)
        top, low = pl.ds(base, bs), pl.ds(pl.multiple_of(base + bs, bs), bs)
        w_buf[parity, top, :half] = re
        w_buf[parity, top, half:] = im
        w_buf[parity, low, :half] = -im
        w_buf[parity, low, half:] = re

    from_col = lax.broadcasted_iota(jnp.int32, (width, width), 0)
    to_col = lax.broadcasted_iota(jnp.int32, (width, width), 1)
    wanted = jnp.where(to_col < half, 2 * to_col, 2 * (to_col - half) + 1)
    order = jnp.where(from_col == wanted, 1.0, 0.0).astype(BF16)

    def enter(b, carry):
        at = pl.ds(pl.multiple_of(b * bs, bs), bs)
        got = jnp.dot(field[at, :], order, preferred_element_type=F32).astype(BF16)
        put_w(0, b, got[:, :half], got[:, half:])
        return carry

    enter(0, 0)
    enter(nb - 1, 0)
    lax.fori_loop(1, nb - 1, enter, 0, unroll=2)
    zero_edge = jnp.zeros((bw, width), BF16)
    for parity in range(2):
        w_buf[parity, :bw, :] = zero_edge
        w_buf[parity, (nb + 1) * bw:, :] = zero_edge

    pl.semaphore_wait(barrier, depth_n - 1 + bits)

    def halo_copy(step, side):
        edge = (1 if side == 0 else nb) * bw
        to = lax.rem(me_d + (depth_n - 1 if side == 0 else 1), depth_n)
        return pltpu.make_async_remote_copy(
            src_ref=w_buf.at[step % 2, pl.ds(edge, bw)],
            dst_ref=halo.at[step, side],
            send_sem=halo_send.at[step, side],
            recv_sem=halo_recv.at[step, side],
            device_id={"depth": to},
            device_id_type=MESH,
        )

    has_above = me_d > 0
    has_below = me_d < depth_n - 1

    def halo_start(step):
        if depth_n == 1:
            return

        @pl.when(has_above)
        def _():
            halo_copy(step, 0).start()

        @pl.when(has_below)
        def _():
            halo_copy(step, 1).start()

    def halo_finish(step):
        if depth_n == 1:
            return

        @pl.when(has_above)
        def _():
            halo_copy(step, 0).wait_send()
            halo_copy(step, 1).wait_recv()
            w_buf[step % 2, :bw, :] = halo[step, 1]

        @pl.when(has_below)
        def _():
            halo_copy(step, 1).wait_send()
            halo_copy(step, 0).wait_recv()
            w_buf[step % 2, (nb + 1) * bw:, :] = halo[step, 0]

    halo_start(0)

    times = out.shape[1]
    lane = lax.broadcasted_iota(jnp.int32, (half, times), 1)

    def basis_of(c, carry):
        n = (c * times + lane).astype(F32)
        y = (freqs[...] * n) * F32(1.0 / NT)
        p = y - jnp.floor(y)
        r = jnp.where(p > 0.5, p - 1.0, p)
        z = r * r
        basis[c, :half, :] = poly(COS_TERMS, z).astype(BF16)
        basis[c, half:, :] = (-(r * poly(SIN_TERMS, z))).astype(BF16)
        return carry

    lax.fori_loop(0, freq_n, basis_of, 0)

    wr = weights[0:1, :]
    wi = weights[1:2, :]
    row_iota = lax.broadcasted_iota(jnp.int32, (bs, half), 0)

    def multiply(step, b):
        parity = step % 2
        near = pl.ds(pl.multiple_of(b * bw, bw), 3 * bw)
        acc = jnp.dot(ops[b], w_buf[parity, near, :], preferred_element_type=F32)
        m, c = acc[:bs], acc[bs:]
        re = m[:, :half] + wr * c[:, :half] - wi * c[:, half:]
        im = m[:, half:] + wr * c[:, half:] + wi * c[:, :half]
        damp = jnp.where(row_iota + (first_row + b * bs) >= floors[step], F32(0.5), F32(1.0))
        re = (damp * re).astype(BF16)
        im = (damp * im).astype(BF16)
        if step == STEPS - 1:
            at = pl.ds(pl.multiple_of(b * bs, bs), bs)
            final[at, :half] = re
            final[at, half:] = im
        else:
            put_w(1 - parity, b, re, im)

    def prepare(b):
        at = pl.ds(pl.multiple_of(b * kc * bs, kc * bs), kc * bs)
        for which, (src, dst) in enumerate(((main_hbm, raw_main), (side_hbm, raw_side))):
            pltpu.make_async_copy(src.at[at], dst.at[at], load_sem.at[which, b]).wait()
            spread[which] = dst[at, :].astype(F32)
            for piece in range(kc):
                ops[b, which * bs:(which + 1) * bs, piece * bs:(piece + 1) * bs] = spread[
                    which, pl.ds(piece, bs, stride=kc), :].astype(BF16)

    prepare(0)
    prepare(nb - 1)
    prepare(1)

    def first_step(b, carry):
        multiply(0, b)

        @pl.when(b + 1 < nb - 1)
        def _():
            prepare(b + 1)

        return carry

    lax.fori_loop(1, nb - 1, first_step, 0)
    halo_finish(0)
    multiply(0, 0)
    multiply(0, nb - 1)
    for step in range(1, STEPS):
        multiply(step, 1)
        multiply(step, 2)
        halo_start(step)

        def inner(b, carry, step=step):
            multiply(step, b)
            return carry

        lax.fori_loop(3, nb - 1, inner, 0, unroll=unroll_of(nb - 4))
        halo_finish(step)
        multiply(step, 0)
        multiply(step, nb - 1)

    here = out.shape[0]
    chunk = min(rows, 1024)

    def pick(owner):
        at = pl.ds(pl.multiple_of(owner * here, here), here)
        local = receivers[at, :] - first_row
        total = jnp.zeros((here, width), F32)
        for base in range(0, rows, chunk):
            marks = [
                jnp.where(local == lax.broadcasted_iota(jnp.int32, local.shape, 1) + (base + sub),
                          1.0, 0.0).astype(BF16)
                for sub in range(0, chunk, local.shape[1])
            ]
            total = total + jnp.dot(jnp.concatenate(marks, axis=1), final[base:base + chunk, :],
                                    preferred_element_type=F32)
        return total

    def pick_copy(off):
        return pltpu.make_async_remote_copy(
            src_ref=picked.at[off - 1],
            dst_ref=pick_in.at[off - 1],
            send_sem=pick_send.at[off - 1],
            recv_sem=pick_recv.at[off - 1],
            device_id={"depth": lax.rem(me_d + off, depth_n)},
            device_id_type=MESH,
        )

    for off in range(1, depth_n):
        picked[off - 1] = pick(lax.rem(me_d + off, depth_n)).astype(BF16)
    for off in range(1, depth_n):
        pick_copy(off).start()
    mine_rows = pick(me_d)
    for off in range(1, depth_n):
        pick_copy(off).wait()
        mine_rows = mine_rows + pick_in[off - 1].astype(F32)
    owned[...] = mine_rows.astype(BF16)

    def chunk_at(part_order, q):
        c = 0
        for t, j in enumerate(part_order):
            c = c + lax.rem(q // (1 << (bits - 1 - t)), 2) * (1 << j)
        return c

    def partial(part, q):
        start, count, part_order = plan[part]
        return jnp.dot(owned[start:start + count, :], basis[chunk_at(part_order, q)],
                       preferred_element_type=F32)

    def offset_of(stage):
        return freq_n - (freq_n >> stage)

    def rs_copy(part, stage):
        size = freq_n >> (stage + 1)
        at = pl.ds(offset_of(stage), size)
        j = plan[part][2][stage]
        return pltpu.make_async_remote_copy(
            src_ref=send_bufs[part].at[at],
            dst_ref=recv_bufs[part].at[at],
            send_sem=rs_send.at[part, stage],
            recv_sem=rs_recv.at[part, stage],
            device_id={"freq": partners[j][1]},
            device_id_type=MESH,
        )

    if bits == 0:
        out[...] = jnp.dot(owned[...], basis[0], preferred_element_type=F32) * factor
        return

    def sweep(size, body):
        def one(q, carry):
            body(q)
            return carry
        lax.fori_loop(0, size, one, 0, unroll=min(2, size))

    size = freq_n // 2
    for part in range(n_parts):
        mine = partners[plan[part][2][0]][0]

        def fill(q, part=part, mine=mine):
            send_bufs[part][q] = partial(part, (1 - mine) * size + q).astype(BF16)

        sweep(size, fill)
    for part in range(n_parts):
        rs_copy(part, 0).start()
    for part in range(n_parts):
        start, count, _ = plan[part]
        mine = partners[plan[part][2][0]][0]

        def keep(q, part=part, mine=mine, start=start, count=count):
            sums[q, start:start + count, :] = partial(part, mine * size + q)

        sweep(size, keep)
    for stage in range(bits):
        size = freq_n >> (stage + 1)
        base = offset_of(stage)
        last = stage == bits - 1
        for part in range(n_parts):
            start, count, part_order = plan[part]
            rs_copy(part, stage).wait()
            at = slice(start, start + count)
            if last:
                out[at, :] = (sums[0, at, :] + recv_bufs[part][base].astype(F32)) * factor
                continue
            nxt = size // 2
            mine = partners[part_order[stage + 1]][0]
            into = offset_of(stage + 1)

            def send(q, part=part, at=at, mine=mine, nxt=nxt, base=base, into=into):
                k = (1 - mine) * nxt + q
                send_bufs[part][into + q] = (
                    sums[k, at, :] + recv_bufs[part][base + k].astype(F32)).astype(BF16)

            sweep(nxt, send)
            rs_copy(part, stage + 1).start()

            def hold(q, part=part, at=at, mine=mine, nxt=nxt, base=base):
                k = mine * nxt + q
                sums[q, at, :] = sums[k, at, :] + recv_bufs[part][base + k].astype(F32)

            sweep(nxt, hold)


def local(depth_n, freq_n, pressure_field, block_main, block_coupled, coupling, frequencies,
          receivers, floors):
    rows, width = pressure_field.shape
    bs = block_main.shape[3]
    half = width // 2
    nb = rows // bs
    bits = freq_n.bit_length() - 1
    here = receivers.shape[0] // depth_n
    times = NT // freq_n
    factor = 1.0 / math.sqrt(frequencies.shape[0])
    plan = plan_of(here, bits)
    weights = coupling.reshape(half, 2).T
    own = lax.dynamic_slice_in_dim(frequencies, lax.axis_index("freq") * half, half)
    freqs = jnp.broadcast_to(own[:, None], (half, times))
    spots = jnp.broadcast_to(receivers[:, None], (receivers.shape[0], bs))
    vmem = pl.BlockSpec(memory_space=pltpu.VMEM)
    hbm = pl.BlockSpec(memory_space=pl.ANY)
    away = max(depth_n - 1, 1)
    slots = max(freq_n - 1, 1)
    return pl.pallas_call(
        functools.partial(kernel, depth_n, freq_n, bits, factor, plan),
        out_shape=jax.ShapeDtypeStruct((here, times), F32),
        in_specs=[vmem, hbm, hbm, vmem, vmem, vmem, pl.BlockSpec(memory_space=pltpu.SMEM)],
        out_specs=vmem,
        scratch_shapes=[
            pltpu.VMEM((rows * 6, bs), BF16),
            pltpu.VMEM((rows * 6, bs), BF16),
            pltpu.VMEM((2, 6 * bs, bs), F32),
            pltpu.VMEM((nb, 2 * bs, 6 * bs), BF16),
            pltpu.VMEM((2, (nb + 2) * 2 * bs, width), BF16),
            pltpu.VMEM((rows, width), BF16),
            pltpu.VMEM((STEPS, 2, 2 * bs, width), BF16),
            pltpu.VMEM((away, here, width), BF16),
            pltpu.VMEM((here, width), BF16),
            pltpu.VMEM((away, here, width), BF16),
            pltpu.VMEM((freq_n, width, times), BF16),
            pltpu.VMEM((max(freq_n // 2, 1), here, times), F32),
            *[pltpu.VMEM((slots, count, times), BF16) for _, count, _ in plan],
            *[pltpu.VMEM((slots, count, times), BF16) for _, count, _ in plan],
            pltpu.SemaphoreType.DMA((2, nb)),
            pltpu.SemaphoreType.DMA((STEPS, 2)),
            pltpu.SemaphoreType.DMA((STEPS, 2)),
            pltpu.SemaphoreType.DMA((away,)),
            pltpu.SemaphoreType.DMA((away,)),
            pltpu.SemaphoreType.DMA((len(plan), max(bits, 1))),
            pltpu.SemaphoreType.DMA((len(plan), max(bits, 1))),
        ],
        compiler_params=pltpu.CompilerParams(
            collective_id=0, has_side_effects=True, vmem_limit_bytes=64 * 1024 * 1024 - 128 * 1024
        ),
    )(
        pressure_field,
        block_main.reshape(rows * 6, bs),
        block_coupled.reshape(rows * 6, bs),
        weights,
        freqs,
        spots,
        floors,
    )


def solution(mesh):
    in_specs = (
        P("depth", "freq"),
        P("depth", None, None, None),
        P("depth", None, None, None),
        P("freq"),
        P(),
        P(),
        P(),
    )
    body = functools.partial(local, mesh.shape["depth"], mesh.shape["freq"])
    return jax.shard_map(body, mesh=mesh, in_specs=in_specs, out_specs=P("depth", "freq"),
                         check_vma=False)
```

profile of v0, /device:TPU:1, one launch (start us, length us, event | category | flops | bytes accessed | tf_op | source)
XLA Modules:
  0.0 134.1 jit_solution(8075187311379970099)
XLA Ops:
  0.0 0.8 dynamic_slice.3
  0.8 0.7 broadcast_in_dim.4.freqs
  1.5 0.8 reshape.13
  2.3 0.6 copy.9
  2.9 1.5 %broadcast_in_dim.5.receivers = s32[512,128]{1,0:T(8,128)} broadcast(s32[512]{0:T(512)} %param.12), dimensions={0} | broadcast | bytes 264192 | tf_op jit(solution)/shard_map/broadcast_in_dim | solution.py:373
  4.4 128.1 %shard_map.73 = f32[256,32]{1,0:T(8,128)} custom-call(bf16[4096,256]{1,0:T(8,128)(2,1)} %field.1, bf16[24576,128]{1,0:T(8,128)(2,1)} %bitcast.3, bf16[24576,128]{1,0:T(8,128)(2,1)} %bitcast.4, f32[2,128]{1,0:T(2,128)} %bitcast.5, f32[128,32]{1,0:T(8,128)} %broadcast_in_dim.4.freqs, s32[512,128]{1,0:T(8,128)} %broadcast_in_dim.5.receivers, s32[4]{0:T(128)} %floors.1), custom_call_target="tpu_custom_call" | custom-call | tf_op jit(solution)/shard_map/pallas_call | solution.py:378
  132.5 1.6 %copy.10 = f32[256,32]{0,1:T(8,128)} copy(f32[256,32]{1,0:T(8,128)} %shard_map.73) | data formatting | bytes 65536 | tf_op jit(solution)/shard_map/pallas_call | solution.py:378
where the time goes:
time: 134 us
  Pallas kernels  128 us (96%)
  local copies, waits for them, and re-layouts  6.01 us (4%)
    pallas_call x1, Pallas kernels, local(): pl.pallas_call(functools.partial(kernel, depth_n, freq_n, bits, factor, p...  128 us

commit v1 on v0

v1 whole, which is shorter than its diff:
```python
import functools
import math

import jax
import jax.numpy as jnp
from jax import lax
from jax.experimental import pallas as pl
from jax.experimental.pallas import tpu as pltpu
from jax.sharding import PartitionSpec as P

NT = 2048
STEPS = 4
NX, NY, NZH = 4, 4, 2
GROUP = 4

COS_TERMS = (1.0, -19.739208221435547, 64.93939208984375, -85.45665740966797,
             60.242130279541016, -26.4046688079834, 7.800131320953369, -1.453112244606018)
SIN_TERMS = (6.2831854820251465, -41.34170150756836, 81.6052474975586, -76.70580291748047,
             42.05775451660156, -15.086565017700195, 3.7813189029693604, -0.6207787394523621)

MESH = pl.DeviceIdType.MESH
F32 = jnp.float32
BF16 = jnp.bfloat16


def poly(terms, z):
    total = jnp.full_like(z, terms[-1])
    for term in terms[-2::-1]:
        total = total * z + F32(term)
    return total


def turn(y):
    p = y - jnp.floor(y)
    r = jnp.where(p > 0.5, p - 1.0, p)
    z = r * r
    return poly(COS_TERMS, z), r * poly(SIN_TERMS, z)


def kernel(depth_n, factor,
           field_hbm, main_hbm, side_hbm, coupling_hbm, freqs_hbm, receivers_hbm, floors, out,
           fbuf, raw_main, raw_side, spread0, spread1, spread2, spread3,
           ops0, ops1, ops2, ops3, w0, w1, final, halo, order_buf,
           coupling, freqs, receivers, weights, spots,
           picked, own, pick_in, sib_own, sib_in, owned,
           coarse, fine, basis_a, basis_b, keep, send1, recv1, send2, recv2, send3, recv3,
           field_sem, load_sem, small_sem, halo_send, halo_recv,
           pick_send, pick_recv, s1_send, s1_recv, s2_send, s2_recv, s3_send, s3_recv):
    rows, width = fbuf.shape
    half = width // 2
    bs = raw_main.shape[1]
    kc = 6
    nb = rows // bs
    bw = 2 * bs
    groups = nb // GROUP
    ops = (ops0, ops1, ops2, ops3)
    spreads = (spread0, spread1, spread2, spread3)
    w_bufs = (w0, w1)
    me_d = lax.axis_index("depth")
    me_f = lax.axis_index("freq")
    first_row = me_d * rows
    core = lax.rem(me_f, 2)
    z = lax.rem(me_f // 2, NZH)
    y = lax.rem(me_f // (2 * NZH), NY)
    x = me_f // (2 * NZH * NY)
    sibling = me_f + 1 - 2 * core

    def chip_of(ox, oy, oz):
        return (lax.rem(x + ox, NX) * NY + lax.rem(y + oy, NY)) * NZH + lax.rem(z + oz, NZH)

    def device_of(ox, oy, oz):
        return {"freq": chip_of(ox, oy, oz) * 2 + core}

    fch = fbuf.shape[0] // groups

    def field_copy(g):
        at = pl.ds(pl.multiple_of(g * fch, fch), fch)
        return pltpu.make_async_copy(field_hbm.at[at], fbuf.at[at], field_sem.at[g])

    def ops_copy(which, b):
        src, dst = ((main_hbm, raw_main), (side_hbm, raw_side))[which]
        at = pl.ds(pl.multiple_of(b * kc * bs, kc * bs), kc * bs)
        return pltpu.make_async_copy(src.at[at], dst.at[at], load_sem.at[which, b])

    small = [pltpu.make_async_copy(src, dst, small_sem.at[i]) for i, (src, dst) in enumerate(
        ((coupling_hbm, coupling), (freqs_hbm, freqs), (receivers_hbm, receivers)))]
    field_copy(0).start()
    small[0].start()

    def start_field(g, carry):
        field_copy(g).start()
        return carry
    lax.fori_loop(1, groups, start_field, 0)

    def start_ops(b, carry):
        ops_copy(0, b).start()
        ops_copy(1, b).start()
        return carry
    lax.fori_loop(0, nb, start_ops, 0)
    small[1].start()
    small[2].start()

    barrier = pltpu.get_barrier_semaphore()
    greeted = 0
    for off in range(1, depth_n):
        pl.semaphore_signal(barrier, inc=1, device_id={"depth": lax.rem(me_d + off, depth_n)},
                            device_id_type=MESH)
        greeted += 1
    peers = [{"freq": sibling}, device_of(0, 0, 1)]
    peers += [device_of(o, 0, 0) for o in range(1, NX)] + [device_of(0, o, 0) for o in range(1, NY)]
    for peer in peers:
        pl.semaphore_signal(barrier, inc=1, device_id=peer, device_id_type=MESH)
        greeted += 1

    from_col = lax.broadcasted_iota(jnp.int32, (width, width), 0)
    to_col = lax.broadcasted_iota(jnp.int32, (width, width), 1)
    wanted = jnp.where(to_col < half, 2 * to_col, 2 * (to_col - half) + 1)
    order_buf[...] = jnp.where(from_col == wanted, 1.0, 0.0).astype(BF16)

    def put_w(w_buf, b, re, im):
        base = pl.multiple_of((b + 1) * bw, bw)
        top, low = pl.ds(base, bs), pl.ds(pl.multiple_of(base + bs, bs), bs)
        w_buf[top, :half] = re
        w_buf[top, half:] = im
        w_buf[low, :half] = -im
        w_buf[low, half:] = re

    zero_edge = jnp.zeros((bw, width), BF16)
    for w_buf in w_bufs:
        w_buf[:bw, :] = zero_edge
        w_buf[(nb + 1) * bw:, :] = zero_edge

    def enter(g):
        field_copy(g).wait()
        at = pl.ds(pl.multiple_of(g * fch, fch), fch)
        got = jnp.dot(fbuf[at, :], order_buf[...], preferred_element_type=F32).astype(BF16)
        for i in range(GROUP):
            one = got[i * bs:(i + 1) * bs, :]
            put_w(w0, g * GROUP + i, one[:, :half], one[:, half:])

    enter(0)
    small[0].wait()
    c16 = jnp.broadcast_to(coupling[...], (16, width))
    high = c16.astype(BF16)
    rest = c16 - high.astype(F32)
    mid = rest.astype(BF16)
    low = (rest - mid.astype(F32)).astype(BF16)
    three = jnp.dot(jnp.concatenate([high, mid, low], axis=0), order_buf[...],
                    preferred_element_type=F32)
    weights[...] = (three[:8] + three[16:24]) + three[32:40]

    def enter_loop(g, carry):
        enter(g)
        return carry
    lax.fori_loop(1, groups, enter_loop, 0)

    pl.semaphore_wait(barrier, greeted)

    def halo_copy(step, side):
        edge = (1 if side == 0 else nb) * bw
        to = lax.rem(me_d + (depth_n - 1 if side == 0 else 1), depth_n)
        return pltpu.make_async_remote_copy(
            src_ref=w_bufs[step % 2].at[pl.ds(edge, bs)],
            dst_ref=halo.at[step, side],
            send_sem=halo_send.at[step, side],
            recv_sem=halo_recv.at[step, side],
            device_id={"depth": to},
            device_id_type=MESH,
        )

    has_above = me_d > 0
    has_below = me_d < depth_n - 1

    def halo_start(step):
        @pl.when(has_above)
        def _():
            halo_copy(step, 0).start()

        @pl.when(has_below)
        def _():
            halo_copy(step, 1).start()

    def halo_finish(step):
        @pl.when(has_above)
        def _():
            halo_copy(step, 0).wait_send()
            halo_copy(step, 1).wait_recv()
            put_w(w_bufs[step % 2], -1, halo[step, 1, :, :half], halo[step, 1, :, half:])

        @pl.when(has_below)
        def _():
            halo_copy(step, 1).wait_send()
            halo_copy(step, 0).wait_recv()
            put_w(w_bufs[step % 2], nb, halo[step, 0, :, :half], halo[step, 0, :, half:])

    halo_start(0)

    row_iota = lax.broadcasted_iota(jnp.int32, (bs, half), 0)

    def multiply(step, g, i):
        b = g * GROUP + i
        near = pl.ds(pl.multiple_of(b * bw, bw), 3 * bw)
        acc = jnp.dot(ops[i][g], w_bufs[step % 2][near, :], preferred_element_type=F32)
        m, c = acc[:bs], acc[bs:]
        wr = weights[0:1, :half]
        wi = weights[0:1, half:]
        re = m[:, :half] + wr * c[:, :half] - wi * c[:, half:]
        im = m[:, half:] + wr * c[:, half:] + wi * c[:, :half]
        damp = jnp.where(row_iota >= floors[step] - (first_row + b * bs), F32(0.5), F32(1.0))
        re = (damp * re).astype(BF16)
        im = (damp * im).astype(BF16)
        if step == STEPS - 1:
            at = pl.ds(pl.multiple_of(b * bs, bs), bs)
            final[at, :half] = re
            final[at, half:] = im
        else:
            put_w(w_bufs[1 - step % 2], b, re, im)

    def prepare(g, i):
        b = g * GROUP + i
        at = pl.ds(pl.multiple_of(b * kc * bs, kc * bs), kc * bs)
        for which, raw in enumerate((raw_main, raw_side)):
            ops_copy(which, b).wait()
            spread = spreads[2 * (i % 2) + which]
            spread[...] = raw[at, :].astype(F32)
            for piece in range(kc):
                ops[i][g, which * bs:(which + 1) * bs, piece * bs:(piece + 1) * bs] = spread[
                    pl.ds(piece, bs, stride=kc), :].astype(BF16)

    prepare(0, 0)
    prepare(0, 1)
    for i in range(1, GROUP):
        if i + 1 < GROUP:
            prepare(0, i + 1)
        else:
            prepare(1, 0)
        multiply(0, 0, i)

    def first_step(g, carry):
        for i in range(GROUP):
            if i + 1 < GROUP:
                prepare(g, i + 1)
            else:
                prepare(g + 1, 0)
            multiply(0, g, i)
        return carry

    lax.fori_loop(1, groups - 1, first_step, 0)
    for i in range(GROUP - 1):
        prepare(groups - 1, i + 1)
        multiply(0, groups - 1, i)
    halo_finish(0)
    multiply(0, 0, 0)
    multiply(0, groups - 1, GROUP - 1)
    small[1].wait()
    small[2].wait()
    for j in range(receivers.shape[0]):
        spots[j * bs:(j + 1) * bs, :] = jnp.broadcast_to(receivers[j:j + 1, :], (bs, bs)).T

    for step in range(1, STEPS):
        halo_start(step)
        for i in range(1, GROUP):
            multiply(step, 0, i)

        def inner(g, carry, step=step):
            for i in range(GROUP):
                multiply(step, g, i)
            return carry

        lax.fori_loop(1, groups - 1, inner, 0, unroll=2)
        for i in range(GROUP - 1):
            multiply(step, groups - 1, i)
        halo_finish(step)
        multiply(step, 0, 0)
        multiply(step, groups - 1, GROUP - 1)

    here = own.shape[0]
    chunk = min(rows, 1024)

    def pick(owner):
        at = pl.ds(pl.multiple_of(owner * here, here), here)
        local = spots[at, :] - first_row
        total = jnp.zeros((here, width), F32)
        for base in range(0, rows, chunk):
            marks = [
                jnp.where(local == lax.broadcasted_iota(jnp.int32, local.shape, 1) + (base + sub),
                          1.0, 0.0).astype(BF16)
                for sub in range(0, chunk, local.shape[1])
            ]
            total = total + jnp.dot(jnp.concatenate(marks, axis=1), final[base:base + chunk, :],
                                    preferred_element_type=F32)
        return total.astype(BF16)

    def move(src, dst, sems, at, to):
        return pltpu.make_async_remote_copy(
            src_ref=src, dst_ref=dst, send_sem=sems[0].at[at], recv_sem=sems[1].at[at],
            device_id=to, device_id_type=MESH)

    pick_sems = (pick_send, pick_recv)
    across = move(picked, pick_in, pick_sems, 0, {"depth": 1 - me_d})
    beside = move(own, sib_own, pick_sems, 1, {"freq": sibling})
    onward = move(pick_in, sib_in, pick_sems, 2, {"freq": sibling})
    picked[...] = pick(1 - me_d)
    across.start()
    own[...] = pick(me_d)
    beside.start()

    chips = NX * NY * NZH
    times = NT // (2 * chips)
    count = lax.broadcasted_iota(jnp.int32, (chips, half), 0).astype(F32)
    late = lax.broadcasted_iota(jnp.int32, (times, half), 0)
    late = (late + core * times).astype(F32)
    for h, line in enumerate((me_f, sibling)):
        tone = freqs[pl.ds(line, 1), :]
        at = slice(h * half, (h + 1) * half)
        cos, sin = turn((tone * count) * F32(1.0 / chips))
        coarse[0, :, at] = cos
        coarse[1, :, at] = -sin
        cos, sin = turn((tone * late) * F32(1.0 / NT))
        fine[0, :, at] = cos
        fine[1, :, at] = sin
    th = times // 2

    def basis_of(q, carry):
        ox, oy = q // NY, lax.rem(q, NY)
        for oz in range(NZH):
            chip = chip_of(ox, oy, oz)
            ca = coarse[0, pl.ds(chip, 1), :]
            na = coarse[1, pl.ds(chip, 1), :]
            for part, (basis, place) in enumerate(
                    ((basis_a, ox * NY + oy), (basis_b, oy * NX + ox))):
                at = pl.ds(pl.multiple_of((place * NZH + oz) * th, th), th)
                cb = fine[0, part * th:(part + 1) * th, :]
                sb = fine[1, part * th:(part + 1) * th, :]
                cos = (ca * cb + na * sb).astype(BF16)
                nsin = (na * cb - ca * sb).astype(BF16)
                for h in range(2):
                    basis[at, 2 * h * half:(2 * h + 1) * half] = cos[:, h * half:(h + 1) * half]
                    basis[at, (2 * h + 1) * half:(2 * h + 2) * half] = nsin[:, h * half:(h + 1) * half]
        return carry

    lax.fori_loop(0, NX * NY, basis_of, 0, unroll=4)

    across.wait()
    onward.start()
    owned[:, :width] = (own[...].astype(F32) + pick_in[...].astype(F32)).astype(BF16)
    beside.wait()
    onward.wait()
    owned[:, width:] = (sib_own[...].astype(F32) + sib_in[...].astype(F32)).astype(BF16)

    slab = NY * NZH * th
    piece = NZH * th
    s1, s2, s3 = (s1_send, s1_recv), (s2_send, s2_recv), (s3_send, s3_recv)

    def over(part, off):
        return device_of(off, 0, 0) if part == 0 else device_of(0, off, 0)

    def series(basis, at):
        return lax.dot_general(basis[at, :], owned[...], (((1,), (1,)), ((), ())),
                               preferred_element_type=F32)

    def first_copy(part, off):
        return move(send1.at[part, off - 1], recv1.at[part, off - 1], s1, (part, off - 1),
                    over(part, off))

    def second_copy(part, off):
        return move(send2.at[part, off - 1], recv2.at[part, off - 1], s2, (part, off - 1),
                    over(1 - part, off))

    def third_copy(part):
        return move(send3.at[part], recv3.at[part], s3, part, device_of(0, 0, 1))

    for part, basis in enumerate((basis_a, basis_b)):
        got = series(basis, slice(slab, NX * slab)).astype(BF16)
        for off in range(1, NX):
            send1[part, off - 1] = got[(off - 1) * slab:off * slab]
        for off in (2, 1, 3):
            first_copy(part, off).start()
    for part, basis in enumerate((basis_a, basis_b)):
        keep[part] = series(basis, slice(0, slab))
    for part in range(2):
        for off in range(1, NX):
            first_copy(part, off).wait()
        for off in (2, 1, 3, 0):
            at = slice(off * piece, (off + 1) * piece)
            total = keep[part, at, :]
            for k in range(NX - 1):
                total = total + recv1[part, k, at, :].astype(F32)
            if off:
                send2[part, off - 1] = total.astype(BF16)
                second_copy(part, off).start()
            else:
                keep[part, at, :] = total
    for part in range(2):
        for off in range(1, NY):
            second_copy(part, off).wait()
        for oz in (1, 0):
            at = slice(oz * th, (oz + 1) * th)
            total = keep[part, at, :]
            for k in range(NY - 1):
                total = total + recv2[part, k, at, :].astype(F32)
            if oz:
                send3[part] = total.astype(BF16)
                third_copy(part).start()
            else:
                keep[part, at, :] = total
    for part in range(2):
        third_copy(part).wait()
        out[part * th:(part + 1) * th, :] = (
            keep[part, :th, :] + recv3[part].astype(F32)) * factor


def local(depth_n, freq_n, pressure_field, block_main, block_coupled, coupling, frequencies,
          receivers, floors):
    rows, width = pressure_field.shape
    bs = block_main.shape[3]
    half = width // 2
    nb = rows // bs
    here = receivers.shape[0] // depth_n
    times = NT // freq_n
    factor = 1.0 / math.sqrt(frequencies.shape[0])
    vmem = pl.BlockSpec(memory_space=pltpu.VMEM)
    hbm = pl.BlockSpec(memory_space=pl.ANY)
    chips = NX * NY * NZH
    th = times // 2
    slab = NY * NZH * th
    dma = pltpu.SemaphoreType.DMA
    result = pl.pallas_call(
        functools.partial(kernel, depth_n, factor),
        out_shape=jax.ShapeDtypeStruct((times, here), F32),
        in_specs=[hbm] * 6 + [pl.BlockSpec(memory_space=pltpu.SMEM)],
        out_specs=vmem,
        scratch_shapes=[
            pltpu.VMEM((rows, width), BF16),
            pltpu.VMEM((rows * 6, bs), BF16),
            pltpu.VMEM((rows * 6, bs), BF16),
            *[pltpu.VMEM((6 * bs, bs), F32) for _ in range(4)],
            *[pltpu.VMEM((nb // GROUP, 2 * bs, 6 * bs), BF16) for _ in range(GROUP)],
            *[pltpu.VMEM(((nb + 2) * 2 * bs, width), BF16) for _ in range(2)],
            pltpu.VMEM((rows, width), BF16),
            pltpu.VMEM((STEPS, 2, bs, width), BF16),
            pltpu.VMEM((width, width), BF16),
            pltpu.VMEM((1, width), F32),
            pltpu.VMEM((frequencies.shape[0] // half, half), F32),
            pltpu.VMEM((receivers.shape[0] // bs, bs), jnp.int32),
            pltpu.VMEM((8, width), F32),
            pltpu.VMEM((receivers.shape[0], bs), jnp.int32),
            pltpu.VMEM((here, width), BF16),
            pltpu.VMEM((here, width), BF16),
            pltpu.VMEM((here, width), BF16),
            pltpu.VMEM((here, width), BF16),
            pltpu.VMEM((here, width), BF16),
            pltpu.VMEM((here, 2 * width), BF16),
            pltpu.VMEM((2, chips, width), F32),
            pltpu.VMEM((2, times, width), F32),
            pltpu.VMEM((NX * slab, 2 * width), BF16),
            pltpu.VMEM((NX * slab, 2 * width), BF16),
            pltpu.VMEM((2, slab, here), F32),
            pltpu.VMEM((2, NX - 1, slab, here), BF16),
            pltpu.VMEM((2, NX - 1, slab, here), BF16),
            pltpu.VMEM((2, NY - 1, NZH * th, here), BF16),
            pltpu.VMEM((2, NY - 1, NZH * th, here), BF16),
            pltpu.VMEM((2, th, here), BF16),
            pltpu.VMEM((2, th, here), BF16),
            dma((nb // GROUP,)),
            dma((2, nb)),
            dma((3,)),
            dma((STEPS, 2)),
            dma((STEPS, 2)),
            dma((3,)),
            dma((3,)),
            dma((2, NX - 1)),
            dma((2, NX - 1)),
            dma((2, NY - 1)),
            dma((2, NY - 1)),
            dma((2,)),
            dma((2,)),
        ],
        compiler_params=pltpu.CompilerParams(
            collective_id=0, has_side_effects=True, vmem_limit_bytes=64 * 1024 * 1024 - 128 * 1024
        ),
    )(
        pressure_field,
        block_main.reshape(rows * 6, bs),
        block_coupled.reshape(rows * 6, bs),
        coupling.reshape(1, width),
        frequencies.reshape(-1, half),
        receivers.reshape(-1, bs),
        floors,
    )
    return result.T


def solution(mesh):
    in_specs = (
        P("depth", "freq"),
        P("depth", None, None, None),
        P("depth", None, None, None),
        P("freq"),
        P(),
        P(),
        P(),
    )
    body = functools.partial(local, mesh.shape["depth"], mesh.shape["freq"])
    return jax.shard_map(body, mesh=mesh, in_specs=in_specs, out_specs=P("depth", "freq"),
                         check_vma=False)
```

time: 134 us -> 63.2 us (0.47); the launches traced: 134 us -> 62 us
  Pallas kernels: 128 us -> 60.6 us
  local copies, waits for them, and re-layouts: 6.01 us -> 1.38 us
    pallas_call x1, Pallas kernels: 128 us -> 60.6 us  [local(): pl.pallas_call(functools.partial(kernel, depth_n, factor), out_shape=jax....]
    broadcast_in_dim x2 -> x0, local copies, waits for them, and re-layouts: 2.21 us -> none  [the longest x1 1.51 us: local(): spots = jnp.broadcast_to(receivers[:, None], (receivers.shape[0], bs))]
    pallas_call x1 -> x0, local copies, waits for them, and re-layouts: 1.59 us -> none  [local(): pl.pallas_call(functools.partial(kernel, depth_n, freq_n, bits, factor, p...]
    reshape x2 -> x0, local copies, waits for them, and re-layouts: 1.45 us -> none  [local(): weights = coupling.reshape(half, 2).T]
    unnamed x0 -> x1, local copies, waits for them, and re-layouts: none -> 1.38 us
where the time goes in v1:
time: 63.2 us; the launch traced here: 62 us
  Pallas kernels  60.6 us (96%)
  local copies, waits for them, and re-layouts  1.38 us (2%)
    pallas_call x1, Pallas kernels, local(): pl.pallas_call(functools.partial(kernel, depth_n, factor), out_shape=jax....  60.6 us
    unnamed x1, local copies, waits for them, and re-layouts  1.38 us

profile of v1, /device:TPU:1, one launch (start us, length us, event | category | flops | bytes accessed | tf_op | source)
XLA Modules:
  0.0 62.0 jit_solution(14004962046194060553)
XLA Ops:
  0.0 60.6 %shard_map.73 = f32[32,256]{1,0:T(8,128)} custom-call(bf16[4096,256]{1,0:T(8,128)(2,1)} %field_hbm.1, bf16[24576,128]{1,0:T(8,128)(2,1)} %bitcast.6, bf16[24576,128]{1,0:T(8,128)(2,1)} %bitcast.7, f32[1,256]{1,0:T(1,128)} %bitcast.11, f32[64,128]{1,0:T(8,128)} %bitcast.9, s32[4,128]{1,0:T(4,128)} %bitcast.10, s32[4]{0:T(128)} %floors.1), custom_call_target="tpu_custom_call" | custom-call | tf_op jit(solution)/shard_map/pallas_call | solution.py:428
  60.6 1.4 %copy.9 = f32[256,32]{0,1:T(8,128)} copy(f32[256,32]{0,1:T(8,128)} %bitcast.8) | data formatting | bytes 65536

commit v2 on v1

--- a/solution.py
+++ b/solution.py
@@ -12,6 +12,7 @@
 STEPS = 4
 NX, NY, NZH = 4, 4, 2
 GROUP = 4
+LATE = 2
 
 COS_TERMS = (1.0, -19.739208221435547, 64.93939208984375, -85.45665740966797,
              60.242130279541016, -26.4046688079834, 7.800131320953369, -1.453112244606018)
@@ -40,7 +41,8 @@
 def kernel(depth_n, factor,
            field_hbm, main_hbm, side_hbm, coupling_hbm, freqs_hbm, receivers_hbm, floors, out,
            fbuf, raw_main, raw_side, spread0, spread1, spread2, spread3,
-           ops0, ops1, ops2, ops3, w0, w1, final, halo, order_buf,
+           ops0, ops1, ops2, ops3, re0, re1, im0, im1, ni0, ni1,
+           final_re, final_im, halo, order_buf,
            coupling, freqs, receivers, weights, spots,
            picked, own, pick_in, sib_own, sib_in, owned,
            coarse, fine, basis_a, basis_b, keep, send1, recv1, send2, recv2, send3, recv3,
@@ -51,11 +53,10 @@
     bs = raw_main.shape[1]
     kc = 6
     nb = rows // bs
-    bw = 2 * bs
     groups = nb // GROUP
     ops = (ops0, ops1, ops2, ops3)
     spreads = (spread0, spread1, spread2, spread3)
-    w_bufs = (w0, w1)
+    re_bufs, im_bufs, ni_bufs = (re0, re1), (im0, im1), (ni0, ni1)
     me_d = lax.axis_index("depth")
     me_f = lax.axis_index("freq")
     first_row = me_d * rows
@@ -77,26 +78,30 @@
         at = pl.ds(pl.multiple_of(g * fch, fch), fch)
         return pltpu.make_async_copy(field_hbm.at[at], fbuf.at[at], field_sem.at[g])
 
-    def ops_copy(which, b):
-        src, dst = ((main_hbm, raw_main), (side_hbm, raw_side))[which]
-        at = pl.ds(pl.multiple_of(b * kc * bs, kc * bs), kc * bs)
-        return pltpu.make_async_copy(src.at[at], dst.at[at], load_sem.at[which, b])
+    def ops_copies(g):
+        count = GROUP * kc * bs
+        at = pl.ds(pl.multiple_of(g * count, count), count)
+        return [pltpu.make_async_copy(src.at[at], dst.at[at], load_sem.at[which, g])
+                for which, (src, dst) in enumerate(((main_hbm, raw_main), (side_hbm, raw_side)))]
 
     small = [pltpu.make_async_copy(src, dst, small_sem.at[i]) for i, (src, dst) in enumerate(
         ((coupling_hbm, coupling), (freqs_hbm, freqs), (receivers_hbm, receivers)))]
     field_copy(0).start()
+    field_copy(groups - 1).start()
     small[0].start()
-
-    def start_field(g, carry):
-        field_copy(g).start()
+    for copy in ops_copies(0):
+        copy.start()
+    field_copy(1).start()
+
+    def start_group(g, carry):
+        field_copy(g + 1).start()
+        for copy in ops_copies(g):
+            copy.start()
         return carry
-    lax.fori_loop(1, groups, start_field, 0)
-
-    def start_ops(b, carry):
-        ops_copy(0, b).start()
-        ops_copy(1, b).start()
-        return carry
-    lax.fori_loop(0, nb, start_ops, 0)
+    lax.fori_loop(1, groups - 2, start_group, 0)
+    for g in (groups - 2, groups - 1):
+        for copy in ops_copies(g):
+            copy.start()
     small[1].start()
     small[2].start()
 
@@ -117,29 +122,29 @@
     wanted = jnp.where(to_col < half, 2 * to_col, 2 * (to_col - half) + 1)
     order_buf[...] = jnp.where(from_col == wanted, 1.0, 0.0).astype(BF16)
 
-    def put_w(w_buf, b, re, im):
-        base = pl.multiple_of((b + 1) * bw, bw)
-        top, low = pl.ds(base, bs), pl.ds(pl.multiple_of(base + bs, bs), bs)
-        w_buf[top, :half] = re
-        w_buf[top, half:] = im
-        w_buf[low, :half] = -im
-        w_buf[low, half:] = re
-
-    zero_edge = jnp.zeros((bw, width), BF16)
-    for w_buf in w_bufs:
-        w_buf[:bw, :] = zero_edge
-        w_buf[(nb + 1) * bw:, :] = zero_edge
+    def put_w(parity, b, re, im):
+        at = pl.ds(pl.multiple_of((b + 1) * bs, bs), bs)
+        re_bufs[parity][at, :] = re
+        im_bufs[parity][at, :] = im
+        ni_bufs[parity][at, :] = -im
+
+    zero_edge = jnp.zeros((bs, half), BF16)
+    for buf in (re0, re1, im0, im1, ni0, ni1):
+        buf[:bs, :] = zero_edge
+        buf[(nb + 1) * bs:, :] = zero_edge
 
     def enter(g):
-        field_copy(g).wait()
         at = pl.ds(pl.multiple_of(g * fch, fch), fch)
         got = jnp.dot(fbuf[at, :], order_buf[...], preferred_element_type=F32).astype(BF16)
         for i in range(GROUP):
             one = got[i * bs:(i + 1) * bs, :]
-            put_w(w0, g * GROUP + i, one[:, :half], one[:, half:])
-
+            put_w(0, g * GROUP + i, one[:, :half], one[:, half:])
+
+    field_copy(0).wait()
+    field_copy(groups - 1).wait()
+    small[0].wait()
     enter(0)
-    small[0].wait()
+    enter(groups - 1)
     c16 = jnp.broadcast_to(coupling[...], (16, width))
     high = c16.astype(BF16)
     rest = c16 - high.astype(F32)
@@ -149,58 +154,42 @@
                     preferred_element_type=F32)
     weights[...] = (three[:8] + three[16:24]) + three[32:40]
 
-    def enter_loop(g, carry):
-        enter(g)
-        return carry
-    lax.fori_loop(1, groups, enter_loop, 0)
-
-    pl.semaphore_wait(barrier, greeted)
-
-    def halo_copy(step, side):
-        edge = (1 if side == 0 else nb) * bw
-        to = lax.rem(me_d + (depth_n - 1 if side == 0 else 1), depth_n)
-        return pltpu.make_async_remote_copy(
-            src_ref=w_bufs[step % 2].at[pl.ds(edge, bs)],
-            dst_ref=halo.at[step, side],
-            send_sem=halo_send.at[step, side],
-            recv_sem=halo_recv.at[step, side],
-            device_id={"depth": to},
+    below = 1 - me_d
+    edge = pl.ds(pl.multiple_of((below * (nb - 1) + 1) * bs, bs), bs)
+
+    def halo_copies(step):
+        return [pltpu.make_async_remote_copy(
+            src_ref=bufs[step % 2].at[edge],
+            dst_ref=halo.at[step, which],
+            send_sem=halo_send.at[step, which],
+            recv_sem=halo_recv.at[step, which],
+            device_id={"depth": 1 - me_d},
             device_id_type=MESH,
-        )
-
-    has_above = me_d > 0
-    has_below = me_d < depth_n - 1
+        ) for which, bufs in enumerate((re_bufs, im_bufs))]
 
     def halo_start(step):
-        @pl.when(has_above)
-        def _():
-            halo_copy(step, 0).start()
-
-        @pl.when(has_below)
-        def _():
-            halo_copy(step, 1).start()
+        for copy in halo_copies(step):
+            copy.start()
 
     def halo_finish(step):
-        @pl.when(has_above)
-        def _():
-            halo_copy(step, 0).wait_send()
-            halo_copy(step, 1).wait_recv()
-            put_w(w_bufs[step % 2], -1, halo[step, 1, :, :half], halo[step, 1, :, half:])
-
-        @pl.when(has_below)
-        def _():
-            halo_copy(step, 1).wait_send()
-            halo_copy(step, 0).wait_recv()
-            put_w(w_bufs[step % 2], nb, halo[step, 0, :, :half], halo[step, 0, :, half:])
-
-    halo_start(0)
+        for copy in halo_copies(step):
+            copy.wait()
+        put_w(step % 2, below * (nb + 1) - 1, halo[step, 0], halo[step, 1])
 
     row_iota = lax.broadcasted_iota(jnp.int32, (bs, half), 0)
 
     def multiply(step, g, i):
         b = g * GROUP + i
-        near = pl.ds(pl.multiple_of(b * bw, bw), 3 * bw)
-        acc = jnp.dot(ops[i][g], w_bufs[step % 2][near, :], preferred_element_type=F32)
+        parity = step % 2
+        acc = None
+        for k in range(3):
+            at = pl.ds(pl.multiple_of((b + k) * bs, bs), bs)
+            re, im, ni = re_bufs[parity][at, :], im_bufs[parity][at, :], ni_bufs[parity][at, :]
+            near = jnp.concatenate([jnp.concatenate([re, im], axis=1),
+                                    jnp.concatenate([ni, re], axis=1)], axis=0)
+            block = jnp.concatenate([ops[i][g, 2 * k], ops[i][g, 2 * k + 1]], axis=1)
+            part = jnp.dot(block, near, preferred_element_type=F32)
+            acc = part if acc is None else acc + part
         m, c = acc[:bs], acc[bs:]
         wr = weights[0:1, :half]
         wi = weights[0:1, half:]
@@ -211,84 +200,88 @@
         im = (damp * im).astype(BF16)
         if step == STEPS - 1:
             at = pl.ds(pl.multiple_of(b * bs, bs), bs)
-            final[at, :half] = re
-            final[at, half:] = im
+            final_re[at, :] = re
+            final_im[at, :] = im
         else:
-            put_w(w_bufs[1 - step % 2], b, re, im)
+            put_w(1 - parity, b, re, im)
 
     def prepare(g, i):
         b = g * GROUP + i
         at = pl.ds(pl.multiple_of(b * kc * bs, kc * bs), kc * bs)
         for which, raw in enumerate((raw_main, raw_side)):
-            ops_copy(which, b).wait()
             spread = spreads[2 * (i % 2) + which]
             spread[...] = raw[at, :].astype(F32)
             for piece in range(kc):
-                ops[i][g, which * bs:(which + 1) * bs, piece * bs:(piece + 1) * bs] = spread[
+                ops[i][g, piece, which * bs:(which + 1) * bs, :] = spread[
                     pl.ds(piece, bs, stride=kc), :].astype(BF16)
 
-    prepare(0, 0)
-    prepare(0, 1)
-    for i in range(1, GROUP):
-        if i + 1 < GROUP:
-            prepare(0, i + 1)
-        else:
-            prepare(1, 0)
-        multiply(0, 0, i)
-
-    def first_step(g, carry):
+    def first_step(g, skip=0, last_field=None):
+        for copy in ops_copies(g + 1):
+            copy.wait()
+        if last_field is None:
+            field_copy(g + 2).wait()
         for i in range(GROUP):
-            if i + 1 < GROUP:
-                prepare(g, i + 1)
-            else:
-                prepare(g + 1, 0)
-            multiply(0, g, i)
+            prepare(g + 1, i)
+            if i >= skip:
+                multiply(0, g, i)
+        if last_field is None:
+            enter(g + 2)
+
+    for copy in ops_copies(0):
+        copy.wait()
+    field_copy(1).wait()
+    for i in range(GROUP):
+        prepare(0, i)
+    enter(1)
+    pl.semaphore_wait(barrier, greeted)
+    halo_start(0)
+    first_step(0, skip=1)
+
+    def first_loop(g, carry):
+        first_step(g)
         return carry
 
-    lax.fori_loop(1, groups - 1, first_step, 0)
-    for i in range(GROUP - 1):
-        prepare(groups - 1, i + 1)
-        multiply(0, groups - 1, i)
+    lax.fori_loop(1, groups - 3, first_loop, 0)
+    first_step(groups - 3, last_field=False)
+    first_step(groups - 2, last_field=False)
     halo_finish(0)
     multiply(0, 0, 0)
     multiply(0, groups - 1, GROUP - 1)
+    for i in range(GROUP - 1):
+        multiply(0, groups - 1, i)
     small[1].wait()
     small[2].wait()
     for j in range(receivers.shape[0]):
-        spots[j * bs:(j + 1) * bs, :] = jnp.broadcast_to(receivers[j:j + 1, :], (bs, bs)).T
+        there = jnp.broadcast_to(receivers[j:j + 1, :], (bs, bs)).T - first_row
+        spots[j * bs:(j + 1) * bs, :] = there.astype(jnp.int16)
 
     for step in range(1, STEPS):
         halo_start(step)
-        for i in range(1, GROUP):
-            multiply(step, 0, i)
-
-        def inner(g, carry, step=step):
-            for i in range(GROUP):
-                multiply(step, g, i)
-            return carry
-
-        lax.fori_loop(1, groups - 1, inner, 0, unroll=2)
-        for i in range(GROUP - 1):
-            multiply(step, groups - 1, i)
+        for b in range(1, nb - 1 - LATE):
+            multiply(step, b // GROUP, b % GROUP)
         halo_finish(step)
         multiply(step, 0, 0)
         multiply(step, groups - 1, GROUP - 1)
+        for b in range(nb - 1 - LATE, nb - 1):
+            multiply(step, b // GROUP, b % GROUP)
 
     here = own.shape[0]
     chunk = min(rows, 1024)
 
     def pick(owner):
         at = pl.ds(pl.multiple_of(owner * here, here), here)
-        local = spots[at, :] - first_row
-        total = jnp.zeros((here, width), F32)
+        local = spots[at, :]
+        lane = lax.broadcasted_iota(jnp.int32, local.shape, 1).astype(jnp.int16)
+        total = None
         for base in range(0, rows, chunk):
             marks = [
-                jnp.where(local == lax.broadcasted_iota(jnp.int32, local.shape, 1) + (base + sub),
-                          1.0, 0.0).astype(BF16)
-                for sub in range(0, chunk, local.shape[1])
+                jnp.where(local == lane + jnp.int16(base + sub), BF16(1.0), BF16(0.0))
+                for sub in range(0, chunk, bs)
             ]
-            total = total + jnp.dot(jnp.concatenate(marks, axis=1), final[base:base + chunk, :],
-                                    preferred_element_type=F32)
+            field = jnp.concatenate(
+                [final_re[base:base + chunk, :], final_im[base:base + chunk, :]], axis=1)
+            part = jnp.dot(jnp.concatenate(marks, axis=1), field, preferred_element_type=F32)
+            total = part if total is None else total + part
         return total.astype(BF16)
 
     def move(src, dst, sems, at, to):
@@ -435,16 +428,17 @@
             pltpu.VMEM((rows * 6, bs), BF16),
             pltpu.VMEM((rows * 6, bs), BF16),
             *[pltpu.VMEM((6 * bs, bs), F32) for _ in range(4)],
-            *[pltpu.VMEM((nb // GROUP, 2 * bs, 6 * bs), BF16) for _ in range(GROUP)],
-            *[pltpu.VMEM(((nb + 2) * 2 * bs, width), BF16) for _ in range(2)],
-            pltpu.VMEM((rows, width), BF16),
-            pltpu.VMEM((STEPS, 2, bs, width), BF16),
+            *[pltpu.VMEM((nb // GROUP, 6, 2 * bs, bs), BF16) for _ in range(GROUP)],
+            *[pltpu.VMEM(((nb + 2) * bs, half), BF16) for _ in range(6)],
+            pltpu.VMEM((rows, half), BF16),
+            pltpu.VMEM((rows, half), BF16),
+            pltpu.VMEM((STEPS, 2, bs, half), BF16),
             pltpu.VMEM((width, width), BF16),
             pltpu.VMEM((1, width), F32),
             pltpu.VMEM((frequencies.shape[0] // half, half), F32),
             pltpu.VMEM((receivers.shape[0] // bs, bs), jnp.int32),
             pltpu.VMEM((8, width), F32),
-            pltpu.VMEM((receivers.shape[0], bs), jnp.int32),
+            pltpu.VMEM((receivers.shape[0], bs), jnp.int16),
             pltpu.VMEM((here, width), BF16),
             pltpu.VMEM((here, width), BF16),
             pltpu.VMEM((here, width), BF16),
@@ -463,7 +457,7 @@
             pltpu.VMEM((2, th, here), BF16),
             pltpu.VMEM((2, th, here), BF16),
             dma((nb // GROUP,)),
-            dma((2, nb)),
+            dma((2, nb // GROUP)),
             dma((3,)),
             dma((STEPS, 2)),
             dma((STEPS, 2)),

time: 63.2 us -> 51.1 us (0.81)
  the two profiles are of different devices: /device:TPU:1 before, /device:TPU:0 now
where the time goes in v2:
time: 51.1 us; the launch traced here: 50.9 us
  Pallas kernels  49.5 us (97%)
  local copies, waits for them, and re-layouts  1.38 us (3%)
    pallas_call x1, Pallas kernels, local(): pl.pallas_call(functools.partial(kernel, depth_n, factor), out_shape=jax....  49.5 us
    unnamed x1, local copies, waits for them, and re-layouts  1.38 us

profile of v2, /device:TPU:0, one launch (start us, length us, event | category | flops | bytes accessed | tf_op | source)
XLA Modules:
  0.0 50.9 jit_solution(3396206814505493318)
XLA Ops:
  0.0 49.5 %shard_map.73 = f32[32,256]{1,0:T(8,128)} custom-call(bf16[4096,256]{1,0:T(8,128)(2,1)} %field_hbm.1, bf16[24576,128]{1,0:T(8,128)(2,1)} %bitcast.6, bf16[24576,128]{1,0:T(8,128)(2,1)} %bitcast.7, f32[1,256]{1,0:T(1,128)} %bitcast.11, f32[64,128]{1,0:T(8,128)} %bitcast.9, s32[4,128]{1,0:T(4,128)} %bitcast.10, s32[4]{0:T(128)} %floors.1), custom_call_target="tpu_custom_call" | custom-call | tf_op jit(solution)/shard_map/pallas_call | solution.py:421
  49.5 1.4 %copy.9 = f32[256,32]{0,1:T(8,128)} copy(f32[256,32]{0,1:T(8,128)} %bitcast.8) | data formatting | bytes 65536

commit v3 on v2

--- a/solution.py
+++ b/solution.py
@@ -40,7 +40,7 @@
 
 def kernel(depth_n, factor,
            field_hbm, main_hbm, side_hbm, coupling_hbm, freqs_hbm, receivers_hbm, floors, out,
-           fbuf, raw_main, raw_side, spread0, spread1, spread2, spread3,
+           fbuf, raw_main, raw_side,
            ops0, ops1, ops2, ops3, re0, re1, im0, im1, ni0, ni1,
            final_re, final_im, halo, order_buf,
            coupling, freqs, receivers, weights, spots,
@@ -50,12 +50,11 @@
            pick_send, pick_recv, s1_send, s1_recv, s2_send, s2_recv, s3_send, s3_recv):
     rows, width = fbuf.shape
     half = width // 2
-    bs = raw_main.shape[1]
+    bs = raw_main.shape[2]
     kc = 6
     nb = rows // bs
     groups = nb // GROUP
     ops = (ops0, ops1, ops2, ops3)
-    spreads = (spread0, spread1, spread2, spread3)
     re_bufs, im_bufs, ni_bufs = (re0, re1), (im0, im1), (ni0, ni1)
     me_d = lax.axis_index("depth")
     me_f = lax.axis_index("freq")
@@ -79,8 +78,7 @@
         return pltpu.make_async_copy(field_hbm.at[at], fbuf.at[at], field_sem.at[g])
 
     def ops_copies(g):
-        count = GROUP * kc * bs
-        at = pl.ds(pl.multiple_of(g * count, count), count)
+        at = pl.ds(g * GROUP, GROUP)
         return [pltpu.make_async_copy(src.at[at], dst.at[at], load_sem.at[which, g])
                 for which, (src, dst) in enumerate(((main_hbm, raw_main), (side_hbm, raw_side)))]
 
@@ -206,14 +204,10 @@
             put_w(1 - parity, b, re, im)
 
     def prepare(g, i):
-        b = g * GROUP + i
-        at = pl.ds(pl.multiple_of(b * kc * bs, kc * bs), kc * bs)
         for which, raw in enumerate((raw_main, raw_side)):
-            spread = spreads[2 * (i % 2) + which]
-            spread[...] = raw[at, :].astype(F32)
             for piece in range(kc):
-                ops[i][g, piece, which * bs:(which + 1) * bs, :] = spread[
-                    pl.ds(piece, bs, stride=kc), :].astype(BF16)
+                ops[i][g, piece, which * bs:(which + 1) * bs, :] = raw.at[
+                    g * GROUP + i][pl.ds(piece, bs, stride=kc), :]
 
     def first_step(g, skip=0, last_field=None):
         for copy in ops_copies(g + 1):
@@ -268,8 +262,8 @@
     here = own.shape[0]
     chunk = min(rows, 1024)
 
-    def pick(owner):
-        at = pl.ds(pl.multiple_of(owner * here, here), here)
+    def pick(owner, first, count):
+        at = pl.ds(pl.multiple_of(owner * here + first, bs), count)
         local = spots[at, :]
         lane = lax.broadcasted_iota(jnp.int32, local.shape, 1).astype(jnp.int16)
         total = None
@@ -290,12 +284,16 @@
             device_id=to, device_id_type=MESH)
 
     pick_sems = (pick_send, pick_recv)
-    across = move(picked, pick_in, pick_sems, 0, {"depth": 1 - me_d})
-    beside = move(own, sib_own, pick_sems, 1, {"freq": sibling})
-    onward = move(pick_in, sib_in, pick_sems, 2, {"freq": sibling})
-    picked[...] = pick(1 - me_d)
-    across.start()
-    own[...] = pick(me_d)
+    across, onward = [], []
+    for h in range(2):
+        at = pl.ds(h * bs, bs)
+        across.append(move(picked.at[at], pick_in.at[at], pick_sems, h, {"depth": 1 - me_d}))
+        onward.append(move(pick_in.at[at], sib_in.at[at], pick_sems, 2 + h, {"freq": sibling}))
+    beside = move(own, sib_own, pick_sems, 4, {"freq": sibling})
+    for h in range(2):
+        picked[h * bs:(h + 1) * bs, :] = pick(1 - me_d, h * bs, bs)
+        across[h].start()
+    own[...] = pick(me_d, 0, here)
     beside.start()
 
     chips = NX * NY * NZH
@@ -334,11 +332,13 @@
 
     lax.fori_loop(0, NX * NY, basis_of, 0, unroll=4)
 
-    across.wait()
-    onward.start()
+    for h in range(2):
+        across[h].wait()
+        onward[h].start()
     owned[:, :width] = (own[...].astype(F32) + pick_in[...].astype(F32)).astype(BF16)
     beside.wait()
-    onward.wait()
+    for h in range(2):
+        onward[h].wait()
     owned[:, width:] = (sib_own[...].astype(F32) + sib_in[...].astype(F32)).astype(BF16)
 
     slab = NY * NZH * th
@@ -352,13 +352,15 @@
         return lax.dot_general(basis[at, :], owned[...], (((1,), (1,)), ((), ())),
                                preferred_element_type=F32)
 
-    def first_copy(part, off):
-        return move(send1.at[part, off - 1], recv1.at[part, off - 1], s1, (part, off - 1),
-                    over(part, off))
-
-    def second_copy(part, off):
-        return move(send2.at[part, off - 1], recv2.at[part, off - 1], s2, (part, off - 1),
-                    over(1 - part, off))
+    def first_copy(part, off, late):
+        at = pl.ds(0, piece) if late else pl.ds(piece, slab - piece)
+        return move(send1.at[part, off - 1, at], recv1.at[part, off - 1, at], s1,
+                    (part, off - 1, late), over(part, off))
+
+    def second_copy(part, off, late):
+        at = pl.ds(0, th) if late else pl.ds(th, piece - th)
+        return move(send2.at[part, off - 1, at], recv2.at[part, off - 1, at], s2,
+                    (part, off - 1, late), over(1 - part, off))
 
     def third_copy(part):
         return move(send3.at[part], recv3.at[part], s3, part, device_of(0, 0, 1))
@@ -367,36 +369,41 @@
         got = series(basis, slice(slab, NX * slab)).astype(BF16)
         for off in range(1, NX):
             send1[part, off - 1] = got[(off - 1) * slab:off * slab]
+    for late in range(2):
         for off in (2, 1, 3):
-            first_copy(part, off).start()
+            for part in range(2):
+                first_copy(part, off, late).start()
     for part, basis in enumerate((basis_a, basis_b)):
         keep[part] = series(basis, slice(0, slab))
+
+    def total_of(recv, count, part, first, size):
+        at = slice(first, first + size)
+        total = keep[part, at, :]
+        for k in range(count):
+            total = total + recv[part, k, at, :].astype(F32)
+        return total
+
     for part in range(2):
         for off in range(1, NX):
-            first_copy(part, off).wait()
-        for off in (2, 1, 3, 0):
-            at = slice(off * piece, (off + 1) * piece)
-            total = keep[part, at, :]
-            for k in range(NX - 1):
-                total = total + recv1[part, k, at, :].astype(F32)
-            if off:
-                send2[part, off - 1] = total.astype(BF16)
-                second_copy(part, off).start()
-            else:
-                keep[part, at, :] = total
+            first_copy(part, off, 0).wait()
+        for off in range(1, NY):
+            send2[part, off - 1] = total_of(recv1, NX - 1, part, off * piece, piece).astype(BF16)
+        for late in range(2):
+            for off in (2, 1, 3):
+                second_copy(part, off, late).start()
+    for part in range(2):
+        for off in range(1, NX):
+            first_copy(part, off, 1).wait()
+        keep[part, :piece, :] = total_of(recv1, NX - 1, part, 0, piece)
     for part in range(2):
         for off in range(1, NY):
-            second_copy(part, off).wait()
-        for oz in (1, 0):
-            at = slice(oz * th, (oz + 1) * th)
-            total = keep[part, at, :]
-            for k in range(NY - 1):
-                total = total + recv2[part, k, at, :].astype(F32)
-            if oz:
-                send3[part] = total.astype(BF16)
-                third_copy(part).start()
-            else:
-                keep[part, at, :] = total
+            second_copy(part, off, 0).wait()
+        send3[part] = total_of(recv2, NY - 1, part, th, th).astype(BF16)
+        third_copy(part).start()
+    for part in range(2):
+        for off in range(1, NY):
+            second_copy(part, off, 1).wait()
+        keep[part, :th, :] = total_of(recv2, NY - 1, part, 0, th)
     for part in range(2):
         third_copy(part).wait()
         out[part * th:(part + 1) * th, :] = (
@@ -425,9 +432,8 @@
         out_specs=vmem,
         scratch_shapes=[
             pltpu.VMEM((rows, width), BF16),
-            pltpu.VMEM((rows * 6, bs), BF16),
-            pltpu.VMEM((rows * 6, bs), BF16),
-            *[pltpu.VMEM((6 * bs, bs), F32) for _ in range(4)],
+            pltpu.VMEM((nb, 6 * bs, bs), BF16),
+            pltpu.VMEM((nb, 6 * bs, bs), BF16),
             *[pltpu.VMEM((nb // GROUP, 6, 2 * bs, bs), BF16) for _ in range(GROUP)],
             *[pltpu.VMEM(((nb + 2) * bs, half), BF16) for _ in range(6)],
             pltpu.VMEM((rows, half), BF16),
@@ -461,12 +467,12 @@
             dma((3,)),
             dma((STEPS, 2)),
             dma((STEPS, 2)),
-            dma((3,)),
-            dma((3,)),
-            dma((2, NX - 1)),
-            dma((2, NX - 1)),
-            dma((2, NY - 1)),
-            dma((2, NY - 1)),
+            dma((5,)),
+            dma((5,)),
+            dma((2, NX - 1, 2)),
+            dma((2, NX - 1, 2)),
+            dma((2, NY - 1, 2)),
+            dma((2, NY - 1, 2)),
             dma((2,)),
             dma((2,)),
         ],
@@ -475,8 +481,8 @@
         ),
     )(
         pressure_field,
-        block_main.reshape(rows * 6, bs),
-        block_coupled.reshape(rows * 6, bs),
+        block_main.reshape(nb, 6 * bs, bs),
+        block_coupled.reshape(nb, 6 * bs, bs),
         coupling.reshape(1, width),
         frequencies.reshape(-1, half),
         receivers.reshape(-1, bs),

time: 51.1 us -> 47.9 us (0.937)
  Pallas kernels: 49.5 us -> 46.3 us
    pallas_call x1, Pallas kernels: 49.5 us -> 46.3 us  [local(): pl.pallas_call(functools.partial(kernel, depth_n, factor), out_shape=jax....]
where the time goes in v3:
time: 47.9 us; the launch traced here: 47.7 us
  Pallas kernels  46.3 us (97%)
  local copies, waits for them, and re-layouts  1.38 us (3%)
    pallas_call x1, Pallas kernels, local(): pl.pallas_call(functools.partial(kernel, depth_n, factor), out_shape=jax....  46.3 us
    unnamed x1, local copies, waits for them, and re-layouts  1.38 us

profile of v3, /device:TPU:0, one launch (start us, length us, event | category | flops | bytes accessed | tf_op | source)
XLA Modules:
  0.0 47.7 jit_solution(9503341821955387278)
XLA Ops:
  0.0 46.3 %shard_map.73 = f32[32,256]{1,0:T(8,128)} custom-call(bf16[4096,256]{1,0:T(8,128)(2,1)} %field_hbm.1, bf16[32,768,128]{2,1,0:T(8,128)(2,1)} %bitcast.6, bf16[32,768,128]{2,1,0:T(8,128)(2,1)} %bitcast.7, f32[1,256]{1,0:T(1,128)} %bitcast.11, f32[64,128]{1,0:T(8,128)} %bitcast.9, s32[4,128]{1,0:T(4,128)} %bitcast.10, s32[4]{0:T(128)} %floors.1), custom_call_target="tpu_custom_call" | custom-call | tf_op jit(solution)/shard_map/pallas_call | solution.py:428
  46.3 1.4 %copy.9 = f32[256,32]{0,1:T(8,128)} copy(f32[256,32]{0,1:T(8,128)} %bitcast.8) | data formatting | bytes 65536

commit v4 on v3

--- a/solution.py
+++ b/solution.py
@@ -39,11 +39,11 @@
 
 
 def kernel(depth_n, factor,
-           field_hbm, main_hbm, side_hbm, coupling_hbm, freqs_hbm, receivers_hbm, floors, out,
+           field_hbm, main_hbm, side_hbm, coupling_hbm, freqs_hbm, receivers_hbm, floors_hbm, out,
            fbuf, raw_main, raw_side,
            ops0, ops1, ops2, ops3, re0, re1, im0, im1, ni0, ni1,
            final_re, final_im, halo, order_buf,
-           coupling, freqs, receivers, weights, spots,
+           coupling, freqs, receivers, floors, weights, near_rows, spots, grab_re, grab_im,
            picked, own, pick_in, sib_own, sib_in, owned,
            coarse, fine, basis_a, basis_b, keep, send1, recv1, send2, recv2, send3, recv3,
            field_sem, load_sem, small_sem, halo_send, halo_recv,
@@ -83,25 +83,27 @@
                 for which, (src, dst) in enumerate(((main_hbm, raw_main), (side_hbm, raw_side)))]
 
     small = [pltpu.make_async_copy(src, dst, small_sem.at[i]) for i, (src, dst) in enumerate(
-        ((coupling_hbm, coupling), (freqs_hbm, freqs), (receivers_hbm, receivers)))]
+        ((coupling_hbm, coupling), (floors_hbm, floors), (freqs_hbm, freqs),
+         (receivers_hbm, receivers)))]
     field_copy(0).start()
     field_copy(groups - 1).start()
     small[0].start()
+    small[1].start()
     for copy in ops_copies(0):
-        copy.start()
+        copy.start(priority=1)
     field_copy(1).start()
 
     def start_group(g, carry):
         field_copy(g + 1).start()
         for copy in ops_copies(g):
-            copy.start()
+            copy.start(priority=1)
         return carry
     lax.fori_loop(1, groups - 2, start_group, 0)
     for g in (groups - 2, groups - 1):
         for copy in ops_copies(g):
-            copy.start()
-    small[1].start()
+            copy.start(priority=1)
     small[2].start()
+    small[3].start()
 
     barrier = pltpu.get_barrier_semaphore()
     greeted = 0
@@ -115,6 +117,9 @@
         pl.semaphore_signal(barrier, inc=1, device_id=peer, device_id_type=MESH)
         greeted += 1
 
+    for buf in (final_re, final_im):
+        buf[rows:, :] = jnp.zeros((buf.shape[0] - rows, half), F32)
+
     from_col = lax.broadcasted_iota(jnp.int32, (width, width), 0)
     to_col = lax.broadcasted_iota(jnp.int32, (width, width), 1)
     wanted = jnp.where(to_col < half, 2 * to_col, 2 * (to_col - half) + 1)
@@ -141,6 +146,7 @@
     field_copy(0).wait()
     field_copy(groups - 1).wait()
     small[0].wait()
+    small[1].wait()
     enter(0)
     enter(groups - 1)
     c16 = jnp.broadcast_to(coupling[...], (16, width))
@@ -176,6 +182,14 @@
 
     row_iota = lax.broadcasted_iota(jnp.int32, (bs, half), 0)
 
+    def piece_of(step, g, i, p):
+        if step > 0:
+            return ops[i][g, p]
+        pair = [raw.at[g * GROUP + i][pl.ds(p, bs, stride=kc), :] for raw in (raw_main, raw_side)]
+        piece = jnp.concatenate(pair, axis=0)
+        ops[i][g, p] = piece
+        return piece
+
     def multiply(step, g, i):
         b = g * GROUP + i
         parity = step % 2
@@ -185,7 +199,8 @@
             re, im, ni = re_bufs[parity][at, :], im_bufs[parity][at, :], ni_bufs[parity][at, :]
             near = jnp.concatenate([jnp.concatenate([re, im], axis=1),
                                     jnp.concatenate([ni, re], axis=1)], axis=0)
-            block = jnp.concatenate([ops[i][g, 2 * k], ops[i][g, 2 * k + 1]], axis=1)
+            block = jnp.concatenate(
+                [piece_of(step, g, i, 2 * k), piece_of(step, g, i, 2 * k + 1)], axis=1)
             part = jnp.dot(block, near, preferred_element_type=F32)
             acc = part if acc is None else acc + part
         m, c = acc[:bs], acc[bs:]
@@ -194,38 +209,27 @@
         re = m[:, :half] + wr * c[:, :half] - wi * c[:, half:]
         im = m[:, half:] + wr * c[:, half:] + wi * c[:, :half]
         damp = jnp.where(row_iota >= floors[step] - (first_row + b * bs), F32(0.5), F32(1.0))
-        re = (damp * re).astype(BF16)
-        im = (damp * im).astype(BF16)
+        re = damp * re
+        im = damp * im
         if step == STEPS - 1:
             at = pl.ds(pl.multiple_of(b * bs, bs), bs)
             final_re[at, :] = re
             final_im[at, :] = im
         else:
-            put_w(1 - parity, b, re, im)
-
-    def prepare(g, i):
-        for which, raw in enumerate((raw_main, raw_side)):
-            for piece in range(kc):
-                ops[i][g, piece, which * bs:(which + 1) * bs, :] = raw.at[
-                    g * GROUP + i][pl.ds(piece, bs, stride=kc), :]
+            put_w(1 - parity, b, re.astype(BF16), im.astype(BF16))
 
     def first_step(g, skip=0, last_field=None):
-        for copy in ops_copies(g + 1):
+        for copy in ops_copies(g):
             copy.wait()
         if last_field is None:
             field_copy(g + 2).wait()
         for i in range(GROUP):
-            prepare(g + 1, i)
             if i >= skip:
                 multiply(0, g, i)
         if last_field is None:
             enter(g + 2)
 
-    for copy in ops_copies(0):
-        copy.wait()
     field_copy(1).wait()
-    for i in range(GROUP):
-        prepare(0, i)
     enter(1)
     pl.semaphore_wait(barrier, greeted)
     halo_start(0)
@@ -238,16 +242,23 @@
     lax.fori_loop(1, groups - 3, first_loop, 0)
     first_step(groups - 3, last_field=False)
     first_step(groups - 2, last_field=False)
+    for copy in ops_copies(groups - 1):
+        copy.wait()
     halo_finish(0)
     multiply(0, 0, 0)
     multiply(0, groups - 1, GROUP - 1)
     for i in range(GROUP - 1):
         multiply(0, groups - 1, i)
-    small[1].wait()
     small[2].wait()
-    for j in range(receivers.shape[0]):
-        there = jnp.broadcast_to(receivers[j:j + 1, :], (bs, bs)).T - first_row
-        spots[j * bs:(j + 1) * bs, :] = there.astype(jnp.int16)
+    small[3].wait()
+    spot = receivers[...] - first_row
+    inside = jnp.logical_and(spot >= 0, spot < rows)
+    near_rows[...] = jnp.where(inside, spot, rows)
+    spot_copies = [
+        pltpu.make_async_copy(near_rows.at[j], spots.at[pl.ds(j * bs, bs)], small_sem.at[4 + j])
+        for j in range(near_rows.shape[0])]
+    for copy in spot_copies:
+        copy.start()
 
     for step in range(1, STEPS):
         halo_start(step)
@@ -260,23 +271,22 @@
             multiply(step, b // GROUP, b % GROUP)
 
     here = own.shape[0]
-    chunk = min(rows, 1024)
-
-    def pick(owner, first, count):
-        at = pl.ds(pl.multiple_of(owner * here + first, bs), count)
-        local = spots[at, :]
-        lane = lax.broadcasted_iota(jnp.int32, local.shape, 1).astype(jnp.int16)
-        total = None
-        for base in range(0, rows, chunk):
-            marks = [
-                jnp.where(local == lane + jnp.int16(base + sub), BF16(1.0), BF16(0.0))
-                for sub in range(0, chunk, bs)
-            ]
-            field = jnp.concatenate(
-                [final_re[base:base + chunk, :], final_im[base:base + chunk, :]], axis=1)
-            part = jnp.dot(jnp.concatenate(marks, axis=1), field, preferred_element_type=F32)
-            total = part if total is None else total + part
-        return total.astype(BF16)
+
+    def pick(owner, h):
+        def take(q, carry):
+            for j in range(16):
+                row = q * 16 + j
+                spot = spots[owner * here + h * bs + row]
+                grab_re[pl.ds(h * bs + row, 1), :] = final_re[pl.ds(spot, 1), :]
+                grab_im[pl.ds(h * bs + row, 1), :] = final_im[pl.ds(spot, 1), :]
+            return carry
+
+        lax.fori_loop(0, bs // 16, take, 0, unroll=2)
+        at = slice(h * bs, (h + 1) * bs)
+        return jnp.concatenate([grab_re[at, :], grab_im[at, :]], axis=1).astype(BF16)
+
+    for copy in spot_copies:
+        copy.wait()
 
     def move(src, dst, sems, at, to):
         return pltpu.make_async_remote_copy(
@@ -291,9 +301,10 @@
         onward.append(move(pick_in.at[at], sib_in.at[at], pick_sems, 2 + h, {"freq": sibling}))
     beside = move(own, sib_own, pick_sems, 4, {"freq": sibling})
     for h in range(2):
-        picked[h * bs:(h + 1) * bs, :] = pick(1 - me_d, h * bs, bs)
+        picked[h * bs:(h + 1) * bs, :] = pick(1 - me_d, h)
         across[h].start()
-    own[...] = pick(me_d, 0, here)
+    for h in range(2):
+        own[h * bs:(h + 1) * bs, :] = pick(me_d, h)
     beside.start()
 
     chips = NX * NY * NZH
@@ -428,7 +439,7 @@
     result = pl.pallas_call(
         functools.partial(kernel, depth_n, factor),
         out_shape=jax.ShapeDtypeStruct((times, here), F32),
-        in_specs=[hbm] * 6 + [pl.BlockSpec(memory_space=pltpu.SMEM)],
+        in_specs=[hbm] * 7,
         out_specs=vmem,
         scratch_shapes=[
             pltpu.VMEM((rows, width), BF16),
@@ -436,15 +447,19 @@
             pltpu.VMEM((nb, 6 * bs, bs), BF16),
             *[pltpu.VMEM((nb // GROUP, 6, 2 * bs, bs), BF16) for _ in range(GROUP)],
             *[pltpu.VMEM(((nb + 2) * bs, half), BF16) for _ in range(6)],
-            pltpu.VMEM((rows, half), BF16),
-            pltpu.VMEM((rows, half), BF16),
+            pltpu.VMEM((rows + 8, half), F32),
+            pltpu.VMEM((rows + 8, half), F32),
             pltpu.VMEM((STEPS, 2, bs, half), BF16),
             pltpu.VMEM((width, width), BF16),
             pltpu.VMEM((1, width), F32),
             pltpu.VMEM((frequencies.shape[0] // half, half), F32),
             pltpu.VMEM((receivers.shape[0] // bs, bs), jnp.int32),
+            pltpu.SMEM((STEPS,), jnp.int32),
             pltpu.VMEM((8, width), F32),
-            pltpu.VMEM((receivers.shape[0], bs), jnp.int16),
+            pltpu.VMEM((receivers.shape[0] // bs, bs), jnp.int32),
+            pltpu.SMEM((receivers.shape[0],), jnp.int32),
+            pltpu.VMEM((here, half), F32),
+            pltpu.VMEM((here, half), F32),
             pltpu.VMEM((here, width), BF16),
             pltpu.VMEM((here, width), BF16),
             pltpu.VMEM((here, width), BF16),
@@ -464,7 +479,7 @@
             pltpu.VMEM((2, th, here), BF16),
             dma((nb // GROUP,)),
             dma((2, nb // GROUP)),
-            dma((3,)),
+            dma((4 + receivers.shape[0] // bs,)),
             dma((STEPS, 2)),
             dma((STEPS, 2)),
             dma((5,)),

time: 47.9 us -> 45.9 us (0.958)
  Pallas kernels: 46.3 us -> 44.4 us
    pallas_call x1, Pallas kernels: 46.3 us -> 44.4 us  [local(): pl.pallas_call(functools.partial(kernel, depth_n, factor), out_shape=jax....]
where the time goes in v4:
time: 45.9 us; the launch traced here: 45.8 us
  Pallas kernels  44.4 us (97%)
  local copies, waits for them, and re-layouts  1.38 us (3%)
    pallas_call x1, Pallas kernels, local(): pl.pallas_call(functools.partial(kernel, depth_n, factor), out_shape=jax....  44.4 us
    unnamed x1, local copies, waits for them, and re-layouts  1.38 us

profile of v4, /device:TPU:0, one launch (start us, length us, event | category | flops | bytes accessed | tf_op | source)
XLA Modules:
  0.0 45.8 jit_solution(5426064031134687762)
XLA Ops:
  0.0 44.4 %shard_map.73 = f32[32,256]{1,0:T(8,128)} custom-call(bf16[4096,256]{1,0:T(8,128)(2,1)} %field_hbm.1, bf16[32,768,128]{2,1,0:T(8,128)(2,1)} %bitcast.6, bf16[32,768,128]{2,1,0:T(8,128)(2,1)} %bitcast.7, f32[1,256]{1,0:T(1,128)} %bitcast.11, f32[64,128]{1,0:T(8,128)} %bitcast.9, s32[4,128]{1,0:T(4,128)} %bitcast.10, s32[4]{0:T(128)} %floors_hbm.1), custom_call_target="tpu_custom_call" | custom-call | tf_op jit(solution)/shard_map/pallas_call | solution.py:439
  44.4 1.4 %copy.9 = f32[256,32]{0,1:T(8,128)} copy(f32[256,32]{0,1:T(8,128)} %bitcast.8) | data formatting | bytes 65536

commit v5 on v4

--- a/solution.py
+++ b/solution.py
@@ -44,7 +44,7 @@
            ops0, ops1, ops2, ops3, re0, re1, im0, im1, ni0, ni1,
            final_re, final_im, halo, order_buf,
            coupling, freqs, receivers, floors, weights, near_rows, spots, grab_re, grab_im,
-           picked, own, pick_in, sib_own, sib_in, owned,
+           picked, own, pick_in, sib_own, owned,
            coarse, fine, basis_a, basis_b, keep, send1, recv1, send2, recv2, send3, recv3,
            field_sem, load_sem, small_sem, halo_send, halo_recv,
            pick_send, pick_recv, s1_send, s1_recv, s2_send, s2_recv, s3_send, s3_recv):
@@ -68,8 +68,8 @@
     def chip_of(ox, oy, oz):
         return (lax.rem(x + ox, NX) * NY + lax.rem(y + oy, NY)) * NZH + lax.rem(z + oz, NZH)
 
-    def device_of(ox, oy, oz):
-        return {"freq": chip_of(ox, oy, oz) * 2 + core}
+    def device_of(ox, oy, oz, oc=0):
+        return {"freq": chip_of(ox, oy, oz) * 2 + lax.rem(core + oc, 2)}
 
     fch = fbuf.shape[0] // groups
 
@@ -107,11 +107,8 @@
 
     barrier = pltpu.get_barrier_semaphore()
     greeted = 0
-    for off in range(1, depth_n):
-        pl.semaphore_signal(barrier, inc=1, device_id={"depth": lax.rem(me_d + off, depth_n)},
-                            device_id_type=MESH)
-        greeted += 1
-    peers = [{"freq": sibling}, device_of(0, 0, 1)]
+    peers = [{"depth": 1 - me_d, "freq": me_f}, {"depth": 1 - me_d, "freq": sibling}]
+    peers += [{"freq": sibling}, device_of(0, 0, 1), device_of(0, 0, 1, 1)]
     peers += [device_of(o, 0, 0) for o in range(1, NX)] + [device_of(0, o, 0) for o in range(1, NY)]
     for peer in peers:
         pl.semaphore_signal(barrier, inc=1, device_id=peer, device_id_type=MESH)
@@ -175,9 +172,11 @@
         for copy in halo_copies(step):
             copy.start()
 
-    def halo_finish(step):
+    def halo_wait(step):
         for copy in halo_copies(step):
             copy.wait()
+
+    def halo_put(step):
         put_w(step % 2, below * (nb + 1) - 1, halo[step, 0], halo[step, 1])
 
     row_iota = lax.broadcasted_iota(jnp.int32, (bs, half), 0)
@@ -244,11 +243,12 @@
     first_step(groups - 2, last_field=False)
     for copy in ops_copies(groups - 1):
         copy.wait()
-    halo_finish(0)
+    halo_wait(0)
+    for i in range(GROUP - 1):
+        multiply(0, groups - 1, i)
+    halo_put(0)
     multiply(0, 0, 0)
     multiply(0, groups - 1, GROUP - 1)
-    for i in range(GROUP - 1):
-        multiply(0, groups - 1, i)
     small[2].wait()
     small[3].wait()
     spot = receivers[...] - first_row
@@ -264,26 +264,28 @@
         halo_start(step)
         for b in range(1, nb - 1 - LATE):
             multiply(step, b // GROUP, b % GROUP)
-        halo_finish(step)
+        halo_wait(step)
+        for b in range(nb - 1 - LATE, nb - 1):
+            multiply(step, b // GROUP, b % GROUP)
+        halo_put(step)
         multiply(step, 0, 0)
         multiply(step, groups - 1, GROUP - 1)
-        for b in range(nb - 1 - LATE, nb - 1):
-            multiply(step, b // GROUP, b % GROUP)
-
-    here = own.shape[0]
-
-    def pick(owner, h):
+
+    here = 2 * bs
+
+    def pick(owner, side):
+        base = owner * here + lax.rem(core + side, 2) * bs
+
         def take(q, carry):
             for j in range(16):
                 row = q * 16 + j
-                spot = spots[owner * here + h * bs + row]
-                grab_re[pl.ds(h * bs + row, 1), :] = final_re[pl.ds(spot, 1), :]
-                grab_im[pl.ds(h * bs + row, 1), :] = final_im[pl.ds(spot, 1), :]
+                spot = spots[base + row]
+                grab_re[pl.ds(row, 1), :] = final_re[pl.ds(spot, 1), :]
+                grab_im[pl.ds(row, 1), :] = final_im[pl.ds(spot, 1), :]
             return carry
 
         lax.fori_loop(0, bs // 16, take, 0, unroll=2)
-        at = slice(h * bs, (h + 1) * bs)
-        return jnp.concatenate([grab_re[at, :], grab_im[at, :]], axis=1).astype(BF16)
+        return jnp.concatenate([grab_re[...], grab_im[...]], axis=1).astype(BF16)
 
     for copy in spot_copies:
         copy.wait()
@@ -294,24 +296,23 @@
             device_id=to, device_id_type=MESH)
 
     pick_sems = (pick_send, pick_recv)
-    across, onward = [], []
-    for h in range(2):
-        at = pl.ds(h * bs, bs)
-        across.append(move(picked.at[at], pick_in.at[at], pick_sems, h, {"depth": 1 - me_d}))
-        onward.append(move(pick_in.at[at], sib_in.at[at], pick_sems, 2 + h, {"freq": sibling}))
-    beside = move(own, sib_own, pick_sems, 4, {"freq": sibling})
-    for h in range(2):
-        picked[h * bs:(h + 1) * bs, :] = pick(1 - me_d, h)
-        across[h].start()
-    for h in range(2):
-        own[h * bs:(h + 1) * bs, :] = pick(me_d, h)
+    across = []
+    for side, line in enumerate((me_f, sibling)):
+        across.append(move(picked.at[side], pick_in.at[side], pick_sems, side,
+                           {"depth": 1 - me_d, "freq": line}))
+    beside = move(own.at[1], sib_own, pick_sems, 2, {"freq": sibling})
+    for side in range(2):
+        picked[side] = pick(1 - me_d, side)
+        across[side].start()
+    own[1] = pick(me_d, 1)
     beside.start()
+    own[0] = pick(me_d, 0)
 
     chips = NX * NY * NZH
     times = NT // (2 * chips)
     count = lax.broadcasted_iota(jnp.int32, (chips, half), 0).astype(F32)
-    late = lax.broadcasted_iota(jnp.int32, (times, half), 0)
-    late = (late + core * times).astype(F32)
+    late = lax.broadcasted_iota(jnp.int32, (2 * times, half), 0)
+    late = jnp.where(late < times, late + core * times, late - core * times).astype(F32)
     for h, line in enumerate((me_f, sibling)):
         tone = freqs[pl.ds(line, 1), :]
         at = slice(h * half, (h + 1) * half)
@@ -321,7 +322,7 @@
         cos, sin = turn((tone * late) * F32(1.0 / NT))
         fine[0, :, at] = cos
         fine[1, :, at] = sin
-    th = times // 2
+    th = times
 
     def basis_of(q, carry):
         ox, oy = q // NY, lax.rem(q, NY)
@@ -341,16 +342,14 @@
                     basis[at, (2 * h + 1) * half:(2 * h + 2) * half] = nsin[:, h * half:(h + 1) * half]
         return carry
 
-    lax.fori_loop(0, NX * NY, basis_of, 0, unroll=4)
-
-    for h in range(2):
-        across[h].wait()
-        onward[h].start()
-    owned[:, :width] = (own[...].astype(F32) + pick_in[...].astype(F32)).astype(BF16)
+    lax.fori_loop(0, NX * NY, basis_of, 0, unroll=2)
+
+    for copy in across:
+        copy.wait()
     beside.wait()
-    for h in range(2):
-        onward[h].wait()
-    owned[:, width:] = (sib_own[...].astype(F32) + sib_in[...].astype(F32)).astype(BF16)
+    for h, one in enumerate((own.at[0], sib_own)):
+        owned[:, h * width:(h + 1) * width] = (
+            one[...].astype(F32) + pick_in[h].astype(F32)).astype(BF16)
 
     slab = NY * NZH * th
     piece = NZH * th
@@ -373,8 +372,8 @@
         return move(send2.at[part, off - 1, at], recv2.at[part, off - 1, at], s2,
                     (part, off - 1, late), over(1 - part, off))
 
-    def third_copy(part):
-        return move(send3.at[part], recv3.at[part], s3, part, device_of(0, 0, 1))
+    third = [move(send3.at[k], recv3.at[k], s3, k, to) for k, to in enumerate(
+        (device_of(0, 0, 1), device_of(0, 0, 1, 1), {"freq": sibling}))]
 
     for part, basis in enumerate((basis_a, basis_b)):
         got = series(basis, slice(slab, NX * slab)).astype(BF16)
@@ -410,15 +409,23 @@
         for off in range(1, NY):
             second_copy(part, off, 0).wait()
         send3[part] = total_of(recv2, NY - 1, part, th, th).astype(BF16)
-        third_copy(part).start()
-    for part in range(2):
+        third[part].start()
+    for part in (1, 0):
         for off in range(1, NY):
             second_copy(part, off, 1).wait()
-        keep[part, :th, :] = total_of(recv2, NY - 1, part, 0, th)
-    for part in range(2):
-        third_copy(part).wait()
-        out[part * th:(part + 1) * th, :] = (
-            keep[part, :th, :] + recv3[part].astype(F32)) * factor
+        total = total_of(recv2, NY - 1, part, 0, th)
+        if part:
+            send3[2] = total.astype(BF16)
+            third[2].start()
+        else:
+            keep[0, :th, :] = total
+    for copy in third:
+        copy.wait()
+    mine = (keep[0, :th, :] + recv3[0].astype(F32)) * factor
+    theirs = (recv3[1].astype(F32) + recv3[2].astype(F32)) * factor
+    first = core == 0
+    out[:, :bs] = jnp.where(first, mine, theirs)
+    out[:, bs:] = jnp.where(first, theirs, mine)
 
 
 def local(depth_n, freq_n, pressure_field, block_main, block_coupled, coupling, frequencies,
@@ -433,7 +440,7 @@
     vmem = pl.BlockSpec(memory_space=pltpu.VMEM)
     hbm = pl.BlockSpec(memory_space=pl.ANY)
     chips = NX * NY * NZH
-    th = times // 2
+    th = times
     slab = NY * NZH * th
     dma = pltpu.SemaphoreType.DMA
     result = pl.pallas_call(
@@ -458,38 +465,37 @@
             pltpu.VMEM((8, width), F32),
             pltpu.VMEM((receivers.shape[0] // bs, bs), jnp.int32),
             pltpu.SMEM((receivers.shape[0],), jnp.int32),
-            pltpu.VMEM((here, half), F32),
-            pltpu.VMEM((here, half), F32),
-            pltpu.VMEM((here, width), BF16),
-            pltpu.VMEM((here, width), BF16),
-            pltpu.VMEM((here, width), BF16),
-            pltpu.VMEM((here, width), BF16),
-            pltpu.VMEM((here, width), BF16),
-            pltpu.VMEM((here, 2 * width), BF16),
+            pltpu.VMEM((bs, half), F32),
+            pltpu.VMEM((bs, half), F32),
+            pltpu.VMEM((2, bs, width), BF16),
+            pltpu.VMEM((2, bs, width), BF16),
+            pltpu.VMEM((2, bs, width), BF16),
+            pltpu.VMEM((bs, width), BF16),
+            pltpu.VMEM((bs, 2 * width), BF16),
             pltpu.VMEM((2, chips, width), F32),
-            pltpu.VMEM((2, times, width), F32),
+            pltpu.VMEM((2, 2 * times, width), F32),
             pltpu.VMEM((NX * slab, 2 * width), BF16),
             pltpu.VMEM((NX * slab, 2 * width), BF16),
-            pltpu.VMEM((2, slab, here), F32),
-            pltpu.VMEM((2, NX - 1, slab, here), BF16),
-            pltpu.VMEM((2, NX - 1, slab, here), BF16),
-            pltpu.VMEM((2, NY - 1, NZH * th, here), BF16),
-            pltpu.VMEM((2, NY - 1, NZH * th, here), BF16),
-            pltpu.VMEM((2, th, here), BF16),
-            pltpu.VMEM((2, th, here), BF16),
+            pltpu.VMEM((2, slab, bs), F32),
+            pltpu.VMEM((2, NX - 1, slab, bs), BF16),
+            pltpu.VMEM((2, NX - 1, slab, bs), BF16),
+            pltpu.VMEM((2, NY - 1, NZH * th, bs), BF16),
+            pltpu.VMEM((2, NY - 1, NZH * th, bs), BF16),
+            pltpu.VMEM((3, th, bs), BF16),
+            pltpu.VMEM((3, th, bs), BF16),
             dma((nb // GROUP,)),
             dma((2, nb // GROUP)),
             dma((4 + receivers.shape[0] // bs,)),
             dma((STEPS, 2)),
             dma((STEPS, 2)),
-            dma((5,)),
-            dma((5,)),
+            dma((3,)),
+            dma((3,)),
             dma((2, NX - 1, 2)),
             dma((2, NX - 1, 2)),
             dma((2, NY - 1, 2)),
             dma((2, NY - 1, 2)),
-            dma((2,)),
-            dma((2,)),
+            dma((3,)),
+            dma((3,)),
         ],
         compiler_params=pltpu.CompilerParams(
             collective_id=0, has_side_effects=True, vmem_limit_bytes=64 * 1024 * 1024 - 128 * 1024

time: 45.9 us -> 45.4 us (0.989)
  the two profiles are of different devices: /device:TPU:0 before, /device:TPU:1 now
where the time goes in v5:
time: 45.4 us; the launch traced here: 45.3 us
  Pallas kernels  43.9 us (97%)
  local copies, waits for them, and re-layouts  1.38 us (3%)
    pallas_call x1, Pallas kernels, local(): pl.pallas_call(functools.partial(kernel, depth_n, factor), out_shape=jax....  43.9 us
    unnamed x1, local copies, waits for them, and re-layouts  1.38 us

profile of v5, /device:TPU:1, one launch (start us, length us, event | category | flops | bytes accessed | tf_op | source)
XLA Modules:
  0.0 45.3 jit_solution(18029768797445882781)
XLA Ops:
  0.0 43.9 %shard_map.73 = f32[32,256]{1,0:T(8,128)} custom-call(bf16[4096,256]{1,0:T(8,128)(2,1)} %field_hbm.1, bf16[32,768,128]{2,1,0:T(8,128)(2,1)} %bitcast.6, bf16[32,768,128]{2,1,0:T(8,128)(2,1)} %bitcast.7, f32[1,256]{1,0:T(1,128)} %bitcast.11, f32[64,128]{1,0:T(8,128)} %bitcast.9, s32[4,128]{1,0:T(4,128)} %bitcast.10, s32[4]{0:T(128)} %floors_hbm.1), custom_call_target="tpu_custom_call" | custom-call | tf_op jit(solution)/shard_map/pallas_call | solution.py:446
  43.9 1.4 %copy.9 = f32[256,32]{0,1:T(8,128)} copy(f32[256,32]{0,1:T(8,128)} %bitcast.8) | data formatting | bytes 65536

commit v6 on v5

--- a/solution.py
+++ b/solution.py
@@ -324,6 +324,9 @@
         fine[1, :, at] = sin
     th = times
 
+    def place_of(off):
+        return lax.rem(off, 2) * 2 + off // 2
+
     def basis_of(q, carry):
         ox, oy = q // NY, lax.rem(q, NY)
         for oz in range(NZH):
@@ -331,7 +334,7 @@
             ca = coarse[0, pl.ds(chip, 1), :]
             na = coarse[1, pl.ds(chip, 1), :]
             for part, (basis, place) in enumerate(
-                    ((basis_a, ox * NY + oy), (basis_b, oy * NX + ox))):
+                    ((basis_a, place_of(oy) * NX + ox), (basis_b, place_of(ox) * NY + oy))):
                 at = pl.ds(pl.multiple_of((place * NZH + oz) * th, th), th)
                 cb = fine[0, part * th:(part + 1) * th, :]
                 sb = fine[1, part * th:(part + 1) * th, :]
@@ -362,10 +365,9 @@
         return lax.dot_general(basis[at, :], owned[...], (((1,), (1,)), ((), ())),
                                preferred_element_type=F32)
 
-    def first_copy(part, off, late):
-        at = pl.ds(0, piece) if late else pl.ds(piece, slab - piece)
-        return move(send1.at[part, off - 1, at], recv1.at[part, off - 1, at], s1,
-                    (part, off - 1, late), over(part, off))
+    def first_copy(part, off, place):
+        return move(send1.at[part, off - 1, place], recv1.at[part, off - 1, place], s1,
+                    (part, off - 1, place), over(part, off))
 
     def second_copy(part, off, late):
         at = pl.ds(0, th) if late else pl.ds(th, piece - th)
@@ -375,53 +377,56 @@
     third = [move(send3.at[k], recv3.at[k], s3, k, to) for k, to in enumerate(
         (device_of(0, 0, 1), device_of(0, 0, 1, 1), {"freq": sibling}))]
 
-    for part, basis in enumerate((basis_a, basis_b)):
-        got = series(basis, slice(slab, NX * slab)).astype(BF16)
-        for off in range(1, NX):
-            send1[part, off - 1] = got[(off - 1) * slab:off * slab]
-    for late in range(2):
-        for off in (2, 1, 3):
-            for part in range(2):
-                first_copy(part, off, late).start()
-    for part, basis in enumerate((basis_a, basis_b)):
-        keep[part] = series(basis, slice(0, slab))
-
-    def total_of(recv, count, part, first, size):
+    for places in ((1,), (2, 3), (0,)):
+        size = NX * piece
+        for part, basis in enumerate((basis_a, basis_b)):
+            got = series(basis, slice(places[0] * size, (places[-1] + 1) * size))
+            for k, place in enumerate(places):
+                keep[part, place] = got[k * size:k * size + piece]
+                for off in range(1, NX):
+                    send1[part, off - 1, place] = got[
+                        k * size + off * piece:k * size + (off + 1) * piece].astype(BF16)
+        for place in places:
+            for off in (2, 1, 3):
+                for part in range(2):
+                    first_copy(part, off, place).start()
+
+    def total_of(recv, count, part, place, first, size):
         at = slice(first, first + size)
-        total = keep[part, at, :]
+        total = keep[part, place, at, :]
         for k in range(count):
-            total = total + recv[part, k, at, :].astype(F32)
+            one = recv[part, k, place, at, :] if recv is recv1 else recv[part, k, at, :]
+            total = total + one.astype(F32)
         return total
 
+    for place, off2 in ((1, 2), (2, 1), (3, 3)):
+        for part in range(2):
+            for off in range(1, NX):
+                first_copy(part, off, place).wait()
+            send2[part, off2 - 1] = total_of(recv1, NX - 1, part, place, 0, piece).astype(BF16)
+            for late in range(2):
+                second_copy(part, off2, late).start()
     for part in range(2):
         for off in range(1, NX):
             first_copy(part, off, 0).wait()
-        for off in range(1, NY):
-            send2[part, off - 1] = total_of(recv1, NX - 1, part, off * piece, piece).astype(BF16)
-        for late in range(2):
-            for off in (2, 1, 3):
-                second_copy(part, off, late).start()
-    for part in range(2):
-        for off in range(1, NX):
-            first_copy(part, off, 1).wait()
-        keep[part, :piece, :] = total_of(recv1, NX - 1, part, 0, piece)
+        keep[part, 0] = total_of(recv1, NX - 1, part, 0, 0, piece)
     for part in range(2):
         for off in range(1, NY):
             second_copy(part, off, 0).wait()
-        send3[part] = total_of(recv2, NY - 1, part, th, th).astype(BF16)
+        send3[part] = total_of(recv2, NY - 1, part, 0, th, th).astype(BF16)
         third[part].start()
     for part in (1, 0):
         for off in range(1, NY):
             second_copy(part, off, 1).wait()
-        total = total_of(recv2, NY - 1, part, 0, th)
+        total = total_of(recv2, NY - 1, part, 0, 0, th)
         if part:
             send3[2] = total.astype(BF16)
             third[2].start()
         else:
-            keep[0, :th, :] = total
+            keep[0, 0, :th, :] = total
     for copy in third:
         copy.wait()
-    mine = (keep[0, :th, :] + recv3[0].astype(F32)) * factor
+    mine = (keep[0, 0, :th, :] + recv3[0].astype(F32)) * factor
     theirs = (recv3[1].astype(F32) + recv3[2].astype(F32)) * factor
     first = core == 0
     out[:, :bs] = jnp.where(first, mine, theirs)
@@ -476,9 +481,9 @@
             pltpu.VMEM((2, 2 * times, width), F32),
             pltpu.VMEM((NX * slab, 2 * width), BF16),
             pltpu.VMEM((NX * slab, 2 * width), BF16),
-            pltpu.VMEM((2, slab, bs), F32),
-            pltpu.VMEM((2, NX - 1, slab, bs), BF16),
-            pltpu.VMEM((2, NX - 1, slab, bs), BF16),
+            pltpu.VMEM((2, NY, NZH * th, bs), F32),
+            pltpu.VMEM((2, NX - 1, NY, NZH * th, bs), BF16),
+            pltpu.VMEM((2, NX - 1, NY, NZH * th, bs), BF16),
             pltpu.VMEM((2, NY - 1, NZH * th, bs), BF16),
             pltpu.VMEM((2, NY - 1, NZH * th, bs), BF16),
             pltpu.VMEM((3, th, bs), BF16),
@@ -490,8 +495,8 @@
             dma((STEPS, 2)),
             dma((3,)),
             dma((3,)),
-            dma((2, NX - 1, 2)),
-            dma((2, NX - 1, 2)),
+            dma((2, NX - 1, NY)),
+            dma((2, NX - 1, NY)),
             dma((2, NY - 1, 2)),
             dma((2, NY - 1, 2)),
             dma((3,)),

time: 45.4 us -> 44.5 us (0.980)
  Pallas kernels: 43.9 us -> 42.9 us
    pallas_call x1, Pallas kernels: 43.9 us -> 42.9 us  [local(): pl.pallas_call(functools.partial(kernel, depth_n, factor), out_shape=jax....]
where the time goes in v6:
time: 44.5 us; the launch traced here: 44.3 us
  Pallas kernels  42.9 us (96%)
  local copies, waits for them, and re-layouts  1.38 us (3%)
    pallas_call x1, Pallas kernels, local(): pl.pallas_call(functools.partial(kernel, depth_n, factor), out_shape=jax....  42.9 us
    unnamed x1, local copies, waits for them, and re-layouts  1.38 us

profile of v6, /device:TPU:1, one launch (start us, length us, event | category | flops | bytes accessed | tf_op | source)
XLA Modules:
  0.0 44.3 jit_solution(3869954566635293586)
XLA Ops:
  0.0 42.9 %shard_map.73 = f32[32,256]{1,0:T(8,128)} custom-call(bf16[4096,256]{1,0:T(8,128)(2,1)} %field_hbm.1, bf16[32,768,128]{2,1,0:T(8,128)(2,1)} %bitcast.6, bf16[32,768,128]{2,1,0:T(8,128)(2,1)} %bitcast.7, f32[1,256]{1,0:T(1,128)} %bitcast.11, f32[64,128]{1,0:T(8,128)} %bitcast.9, s32[4,128]{1,0:T(4,128)} %bitcast.10, s32[4]{0:T(128)} %floors_hbm.1), custom_call_target="tpu_custom_call" | custom-call | tf_op jit(solution)/shard_map/pallas_call | solution.py:451
  42.9 1.4 %copy.9 = f32[256,32]{0,1:T(8,128)} copy(f32[256,32]{0,1:T(8,128)} %bitcast.8) | data formatting | bytes 65536

commit v7 on v6

--- a/solution.py
+++ b/solution.py
@@ -45,9 +45,9 @@
            final_re, final_im, halo, order_buf,
            coupling, freqs, receivers, floors, weights, near_rows, spots, grab_re, grab_im,
            picked, own, pick_in, sib_own, owned,
-           coarse, fine, basis_a, basis_b, keep, send1, recv1, send2, recv2, send3, recv3,
+           coarse, fine, basis_a, basis_b, keep, send1, recv1, send2, recv2,
            field_sem, load_sem, small_sem, halo_send, halo_recv,
-           pick_send, pick_recv, s1_send, s1_recv, s2_send, s2_recv, s3_send, s3_recv):
+           pick_send, pick_recv, s1_send, s1_recv, s2_send, s2_recv):
     rows, width = fbuf.shape
     half = width // 2
     bs = raw_main.shape[2]
@@ -108,8 +108,9 @@
     barrier = pltpu.get_barrier_semaphore()
     greeted = 0
     peers = [{"depth": 1 - me_d, "freq": me_f}, {"depth": 1 - me_d, "freq": sibling}]
-    peers += [{"freq": sibling}, device_of(0, 0, 1), device_of(0, 0, 1, 1)]
-    peers += [device_of(o, 0, 0) for o in range(1, NX)] + [device_of(0, o, 0) for o in range(1, NY)]
+    peers += [device_of(o, 0, 0) for o in range(1, NX)]
+    peers += [device_of(0, o, oz) for o in range(NY) for oz in range(NZH) if o or oz]
+    peers += [device_of(o, 0, oz, 1) for o in range(NX) for oz in range(NZH)]
     for peer in peers:
         pl.semaphore_signal(barrier, inc=1, device_id=peer, device_id_type=MESH)
         greeted += 1
@@ -356,7 +357,7 @@
 
     slab = NY * NZH * th
     piece = NZH * th
-    s1, s2, s3 = (s1_send, s1_recv), (s2_send, s2_recv), (s3_send, s3_recv)
+    s1, s2 = (s1_send, s1_recv), (s2_send, s2_recv)
 
     def over(part, off):
         return device_of(off, 0, 0) if part == 0 else device_of(0, off, 0)
@@ -369,13 +370,11 @@
         return move(send1.at[part, off - 1, place], recv1.at[part, off - 1, place], s1,
                     (part, off - 1, place), over(part, off))
 
-    def second_copy(part, off, late):
-        at = pl.ds(0, th) if late else pl.ds(th, piece - th)
-        return move(send2.at[part, off - 1, at], recv2.at[part, off - 1, at], s2,
-                    (part, off - 1, late), over(1 - part, off))
-
-    third = [move(send3.at[k], recv3.at[k], s3, k, to) for k, to in enumerate(
-        (device_of(0, 0, 1), device_of(0, 0, 1, 1), {"freq": sibling}))]
+    def second_copy(part, place, oz):
+        off = (place % 2) * 2 + place // 2
+        to = device_of(off, 0, oz, 1) if part else device_of(0, off, oz)
+        return move(send2.at[part, place, oz], recv2.at[part, place, oz], s2,
+                    (part, place, oz), to)
 
     for places in ((1,), (2, 3), (0,)):
         size = NX * piece
@@ -391,43 +390,29 @@
                 for part in range(2):
                     first_copy(part, off, place).start()
 
-    def total_of(recv, count, part, place, first, size):
-        at = slice(first, first + size)
-        total = keep[part, place, at, :]
-        for k in range(count):
-            one = recv[part, k, place, at, :] if recv is recv1 else recv[part, k, at, :]
-            total = total + one.astype(F32)
-        return total
-
-    for place, off2 in ((1, 2), (2, 1), (3, 3)):
+    for place in (1, 2, 3, 0):
         for part in range(2):
             for off in range(1, NX):
                 first_copy(part, off, place).wait()
-            send2[part, off2 - 1] = total_of(recv1, NX - 1, part, place, 0, piece).astype(BF16)
-            for late in range(2):
-                second_copy(part, off2, late).start()
-    for part in range(2):
-        for off in range(1, NX):
-            first_copy(part, off, 0).wait()
-        keep[part, 0] = total_of(recv1, NX - 1, part, 0, 0, piece)
-    for part in range(2):
-        for off in range(1, NY):
-            second_copy(part, off, 0).wait()
-        send3[part] = total_of(recv2, NY - 1, part, 0, th, th).astype(BF16)
-        third[part].start()
-    for part in (1, 0):
-        for off in range(1, NY):
-            second_copy(part, off, 1).wait()
-        total = total_of(recv2, NY - 1, part, 0, 0, th)
-        if part:
-            send3[2] = total.astype(BF16)
-            third[2].start()
-        else:
-            keep[0, 0, :th, :] = total
-    for copy in third:
-        copy.wait()
-    mine = (keep[0, 0, :th, :] + recv3[0].astype(F32)) * factor
-    theirs = (recv3[1].astype(F32) + recv3[2].astype(F32)) * factor
+            total = keep[part, place]
+            for k in range(NX - 1):
+                total = total + recv1[part, k, place].astype(F32)
+            for oz in (1, 0):
+                one = total[oz * th:(oz + 1) * th]
+                if part or place or oz:
+                    send2[part, place, oz] = one.astype(BF16)
+                    second_copy(part, place, oz).start()
+                else:
+                    keep[0, 0, :th, :] = one
+    came = [(part, place, oz) for part in range(2) for place in range(NY) for oz in range(NZH)
+            if part or place or oz]
+    for at in came:
+        second_copy(*at).wait()
+    both = [keep[0, 0, :th, :], None]
+    for part, place, oz in came:
+        one = recv2[part, place, oz].astype(F32)
+        both[part] = one if both[part] is None else both[part] + one
+    mine, theirs = both[0] * factor, both[1] * factor
     first = core == 0
     out[:, :bs] = jnp.where(first, mine, theirs)
     out[:, bs:] = jnp.where(first, theirs, mine)
@@ -484,10 +469,8 @@
             pltpu.VMEM((2, NY, NZH * th, bs), F32),
             pltpu.VMEM((2, NX - 1, NY, NZH * th, bs), BF16),
             pltpu.VMEM((2, NX - 1, NY, NZH * th, bs), BF16),
-            pltpu.VMEM((2, NY - 1, NZH * th, bs), BF16),
-            pltpu.VMEM((2, NY - 1, NZH * th, bs), BF16),
-            pltpu.VMEM((3, th, bs), BF16),
-            pltpu.VMEM((3, th, bs), BF16),
+            pltpu.VMEM((2, NY, NZH, th, bs), BF16),
+            pltpu.VMEM((2, NY, NZH, th, bs), BF16),
             dma((nb // GROUP,)),
             dma((2, nb // GROUP)),
             dma((4 + receivers.shape[0] // bs,)),
@@ -497,10 +480,8 @@
             dma((3,)),
             dma((2, NX - 1, NY)),
             dma((2, NX - 1, NY)),
-            dma((2, NY - 1, 2)),
-            dma((2, NY - 1, 2)),
-            dma((3,)),
-            dma((3,)),
+            dma((2, NY, NZH)),
+            dma((2, NY, NZH)),
         ],
         compiler_params=pltpu.CompilerParams(
             collective_id=0, has_side_effects=True, vmem_limit_bytes=64 * 1024 * 1024 - 128 * 1024

time: 44.5 us -> 42.7 us (0.960)
  Pallas kernels: 42.9 us -> 41.2 us
    pallas_call x1, Pallas kernels: 42.9 us -> 41.2 us  [local(): pl.pallas_call(functools.partial(kernel, depth_n, factor), out_shape=jax....]
where the time goes in v7:
time: 42.7 us; the launch traced here: 42.6 us
  Pallas kernels  41.2 us (96%)
  local copies, waits for them, and re-layouts  1.38 us (3%)
    pallas_call x1, Pallas kernels, local(): pl.pallas_call(functools.partial(kernel, depth_n, factor), out_shape=jax....  41.2 us
    unnamed x1, local copies, waits for them, and re-layouts  1.38 us

profile of v7, /device:TPU:1, one launch (start us, length us, event | category | flops | bytes accessed | tf_op | source)
XLA Modules:
  0.0 42.6 jit_solution(5633286984887085674)
XLA Ops:
  0.0 41.2 %shard_map.73 = f32[32,256]{1,0:T(8,128)} custom-call(bf16[4096,256]{1,0:T(8,128)(2,1)} %field_hbm.1, bf16[32,768,128]{2,1,0:T(8,128)(2,1)} %bitcast.6, bf16[32,768,128]{2,1,0:T(8,128)(2,1)} %bitcast.7, f32[1,256]{1,0:T(1,128)} %bitcast.11, f32[64,128]{1,0:T(8,128)} %bitcast.9, s32[4,128]{1,0:T(4,128)} %bitcast.10, s32[4]{0:T(128)} %floors_hbm.1), custom_call_target="tpu_custom_call" | custom-call | tf_op jit(solution)/shard_map/pallas_call | solution.py:436
  41.2 1.4 %copy.9 = f32[256,32]{0,1:T(8,128)} copy(f32[256,32]{0,1:T(8,128)} %bitcast.8) | data formatting | bytes 65536

commit v8 on v7

--- a/solution.py
+++ b/solution.py
@@ -231,15 +231,16 @@
 
     field_copy(1).wait()
     enter(1)
+    first_step(0, skip=1)
+    first_step(1)
     pl.semaphore_wait(barrier, greeted)
     halo_start(0)
-    first_step(0, skip=1)
 
     def first_loop(g, carry):
         first_step(g)
         return carry
 
-    lax.fori_loop(1, groups - 3, first_loop, 0)
+    lax.fori_loop(2, groups - 3, first_loop, 0)
     first_step(groups - 3, last_field=False)
     first_step(groups - 2, last_field=False)
     for copy in ops_copies(groups - 1):

time: 42.7 us -> 42.6 us (level)
  no operation moved by 1% of the time
where the time goes in v8:
time: 42.6 us; the launch traced here: 42.4 us
  Pallas kernels  41 us (96%)
  local copies, waits for them, and re-layouts  1.38 us (3%)
    pallas_call x1, Pallas kernels, local(): pl.pallas_call(functools.partial(kernel, depth_n, factor), out_shape=jax....  41 us
    unnamed x1, local copies, waits for them, and re-layouts  1.38 us

profile of v8, /device:TPU:1, one launch (start us, length us, event | category | flops | bytes accessed | tf_op | source)
XLA Modules:
  0.0 42.4 jit_solution(16276299639409299607)
XLA Ops:
  0.0 41.0 %shard_map.73 = f32[32,256]{1,0:T(8,128)} custom-call(bf16[4096,256]{1,0:T(8,128)(2,1)} %field_hbm.1, bf16[32,768,128]{2,1,0:T(8,128)(2,1)} %bitcast.6, bf16[32,768,128]{2,1,0:T(8,128)(2,1)} %bitcast.7, f32[1,256]{1,0:T(1,128)} %bitcast.11, f32[64,128]{1,0:T(8,128)} %bitcast.9, s32[4,128]{1,0:T(4,128)} %bitcast.10, s32[4]{0:T(128)} %floors_hbm.1), custom_call_target="tpu_custom_call" | custom-call | tf_op jit(solution)/shard_map/pallas_call | solution.py:437
  41.0 1.4 %copy.9 = f32[256,32]{0,1:T(8,128)} copy(f32[256,32]{0,1:T(8,128)} %bitcast.8) | data formatting | bytes 65536
